TPU v7x, 256 devices: a whole 4x4x8 slice. The times are simulated.
256 devices in a mesh: seq: 64 (over z, y, core), head: 4 (over x).
Axes of the slice: x: 4, y: 4, z: 8, core: 2. Of those that a mesh axis runs over, the one named last changes fastest.
Arguments:
- layer_in: bfloat16 [32768, 2048], P('seq', 'head'), may hold values from -6 to 6
- query_weight: bfloat16 [2048, 1024], P(None, 'head'), may hold values from -0.125 to 0.125
- key_weight: bfloat16 [2048, 1024], P(None, 'head'), may hold values from -0.125 to 0.125
- value_weight: bfloat16 [2048, 1024], P(None, 'head'), may hold values from -0.125 to 0.125
- gate_weight: bfloat16 [2048, 1024], P(None, 'head'), may hold values from -0.125 to 0.125
- beta_weight: bfloat16 [2048, 8], P(None, 'head'), may hold values from -0.125 to 0.125
- decay_weight: bfloat16 [2048, 8], P(None, 'head'), may hold values from -0.125 to 0.125
- conv_weight: float32 [4, 3, 1024], P(None, None, 'head'), may hold values from -3 to 3
- decay_log: float32 [8], P('head'), as said below
- beta_bias: float32 [8], P('head'), as said below
- decay_bias: float32 [8], P('head'), may hold values from -1 to 1
- norm_gain: float32 [128], replicated, may hold values from 0.1 to 1.9
- out_weight: bfloat16 [1024, 2048], P('head'), may hold values from -0.1875 to 0.1875
Outputs:
- layer_out: bfloat16 [32768, 2048], P('seq', 'head')
Inputs may be any that keep to these rules, and one draw needn't show every extreme that they name: decay_log lies between log(0.1 / 32768) and log(0.05). beta_bias lies between log(0.5 * 128 / 32768) and 1.
All inputs are finite; a program needn't handle non-finite values.
Results may differ from a plain program's by a relative error of at most 0.0049.
Values may be sent and summed in bfloat16 or wider, within the bound.
A program may use at most 128 MiB of HBM per device.

v0:
```python
import jax
import jax.numpy as jnp
from jax import lax
from jax.sharding import Mesh
from jax.sharding import PartitionSpec as P

BLOCK = 128
SEQ = ("seq_0", "seq_1", "seq_2")


exact_mode = lax.Precision.HIGHEST
norm_floor = 0.0001


def passed_along(value, axis, steps):
    count = lax.axis_size(axis)
    leading, last = (max(0, -steps), min(count, count - steps))
    return lax.ppermute(value, axis, [(source, source + steps) for source in range(leading, last)])


def neutral_like(value, identity):
    return jax.tree.map(
        lambda part, zero: jnp.zeros_like(part) + jnp.asarray(zero, part.dtype), value, identity
    )


def carried_in(value, axes, combine, identity):
    before = start = neutral_like(value, identity)
    subtotal = value
    for axis in reversed(axes):
        length, mine = (lax.axis_size(axis), lax.axis_index(axis))
        pieces = jax.tree.map(lambda part: lax.all_gather(part, axis), subtotal)
        inside, subtotal = (start, start)
        for k in range(length):
            passed = k < mine
            subtotal = combine(subtotal, jax.tree.map(lambda part: part[k], pieces))
            inside = jax.tree.map(lambda new, old: jnp.where(passed, new, old), subtotal, inside)
        before = combine(inside, before)
    return before


def copy_for_each(value, axis):
    length = lax.axis_size(axis)
    return lax.all_to_all(
        jnp.broadcast_to(value[None], (length, *value.shape)), axis, 0, 0, tiled=True
    )


def in_order(tiles, dim):
    tiles = jnp.moveaxis(tiles, 0, dim)
    dims = tiles.shape
    return tiles.reshape(*dims[:dim], dims[dim] * dims[dim + 1], *dims[dim + 2 :])


def collect(value, axis, dim):
    tiles = copy_for_each(value, axis)
    return in_order(tiles, dim)


def causal_conv(values, earlier, kernel):
    reach_back = kernel.shape[0] - 1
    tokens = values.shape[0]
    extended = jnp.concatenate([earlier, values], axis=0)
    summed = kernel[0] * values
    for offset in range(1, reach_back + 1):
        summed = (
            summed + kernel[offset] * extended[reach_back - offset : reach_back - offset + tokens]
        )
    return jax.nn.silu(summed)


def unit_rows(values):
    return values * lax.rsqrt(jnp.sum(values * values, axis=-1, keepdims=True) + 1.0)


def unit_lower_inverse(system):
    length = system.shape[-1]
    row_index = lax.broadcasted_iota(jnp.int32, (length, length), 0)
    col_index = lax.broadcasted_iota(jnp.int32, (length, length), 1)
    inverse = jnp.broadcast_to(jnp.eye(length, dtype=jnp.float32), system.shape)
    width = 1
    while width < length:
        same_pair = row_index // (2 * width) == col_index // (2 * width)
        lower_half = row_index // width > col_index // width
        linking = jnp.where(same_pair & lower_half, system, 0.0)
        middle = lax.optimization_barrier(
            jnp.einsum("...rs,...st->...rt", linking, inverse, precision=exact_mode)
        )
        update = lax.optimization_barrier(
            jnp.einsum("...rs,...st->...rt", inverse, middle, precision=exact_mode)
        )
        inverse = inverse - update
        width = width * 2
    return inverse


def block_terms(queries, key_rows, values, beta_gate, log_decay):
    length = log_decay.shape[-1]
    running = jnp.cumsum(log_decay, axis=-1)
    row_index = lax.broadcasted_iota(jnp.int32, (length, length), 0)
    col_index = lax.broadcasted_iota(jnp.int32, (length, length), 1)
    within = row_index >= col_index
    before = row_index > col_index
    spread = running[..., :, None] - running[..., None, :]
    decay_matrix = jnp.where(within, jnp.exp(jnp.minimum(spread, 0.0)), 0.0)
    key_gram = jnp.einsum("...rd,...sd->...rs", key_rows, key_rows, precision=exact_mode)
    lower_part = jnp.where(before, beta_gate[..., :, None] * decay_matrix * key_gram, 0.0)
    system = lower_part + jnp.eye(length, dtype=jnp.float32)
    growth = jnp.exp(running)
    right_side = jnp.concatenate(
        [beta_gate[..., None] * values, (beta_gate * growth)[..., None] * key_rows], axis=-1
    )
    solved = jnp.einsum(
        "...rs,...se->...re", unit_lower_inverse(system), right_side, precision=exact_mode
    )
    value_dim = values.shape[-1]
    fixed_rows = solved[..., :value_dim]
    erased = solved[..., value_dim:]
    query_key = jnp.einsum("...rd,...sd->...rs", queries, key_rows, precision=exact_mode)
    mixing = jnp.where(within, decay_matrix * query_key, 0.0)
    local_out = jnp.einsum("...rs,...se->...re", mixing, fixed_rows, precision=exact_mode)
    removed = lax.optimization_barrier(
        jnp.einsum("...rs,...sd->...rd", mixing, erased, precision=exact_mode)
    )
    reader = growth[..., None] * queries - removed
    tail_decay = jnp.exp(running[..., -1:] - running)
    weighted = tail_decay[..., None] * key_rows
    key_dim = key_rows.shape[-1]
    lost_part = lax.optimization_barrier(
        jnp.einsum("...bd,...be->...de", weighted, erased, precision=exact_mode)
    )
    transit = (
        jnp.exp(running[..., -1])[..., None, None] * jnp.eye(key_dim, dtype=jnp.float32) - lost_part
    )
    carried = jnp.einsum("...bd,...be->...de", weighted, fixed_rows, precision=exact_mode)
    return (local_out, reader, transit, carried)


def compose(earlier, later_map):
    joined = jnp.einsum("...de,...ef->...df", later_map[0], earlier[0], precision=exact_mode)
    moved = (
        jnp.einsum("...de,...ef->...df", later_map[0], earlier[1], precision=exact_mode)
        + later_map[1]
    )
    return (joined, moved)


def on_device(
    layer_in,
    query_weight,
    key_weight,
    value_weight,
    gate_weight,
    beta_weight,
    decay_weight,
    conv_weight,
    decay_log,
    beta_bias,
    decay_bias,
    norm_gain,
    out_weight,
):
    tokens = layer_in.shape[0]
    head_count = beta_weight.shape[1]
    head_dim = query_weight.shape[1] // head_count
    weights = (query_weight, key_weight, value_weight, gate_weight, beta_weight, decay_weight)
    shard_piece = lax.all_gather(layer_in, "head", axis=1, tiled=True)
    query_raw, key_raw, value_raw, gate_raw, beta_raw, decay_raw = tuple(
        (jnp.dot(shard_piece, weight, preferred_element_type=jnp.float32) for weight in weights)
    )
    reach_back = conv_weight.shape[0] - 1
    channels = query_raw.shape[1]
    last_rows = jnp.concatenate(
        [
            query_raw[tokens - reach_back :],
            key_raw[tokens - reach_back :],
            value_raw[tokens - reach_back :],
        ],
        axis=1,
    )
    prior_rows = passed_along(last_rows, SEQ, 1)
    mixed_query = causal_conv(query_raw, prior_rows[:, :channels], conv_weight[:, 0])
    mixed_key = causal_conv(key_raw, prior_rows[:, channels : 2 * channels], conv_weight[:, 1])
    mixed_value = causal_conv(value_raw, prior_rows[:, 2 * channels :], conv_weight[:, 2])
    queries = unit_rows(mixed_query.reshape(tokens, head_count, head_dim))
    key_rows = unit_rows(mixed_key.reshape(tokens, head_count, head_dim))
    values = mixed_value.reshape(tokens, head_count, head_dim)
    beta_gate = jax.nn.sigmoid(beta_raw + beta_bias)
    log_decay = -jnp.exp(decay_log) * jax.nn.softplus(decay_raw + decay_bias)
    blocks = tokens // BLOCK

    def arrange(array):
        return array.reshape(blocks, BLOCK, head_count, head_dim).transpose(0, 2, 1, 3)

    def arrange_gate(array):
        return array.reshape(blocks, BLOCK, head_count).transpose(0, 2, 1)

    local_out, reader, transit, carried = block_terms(
        arrange(queries),
        arrange(key_rows),
        arrange(values),
        arrange_gate(beta_gate),
        arrange_gate(log_decay),
    )
    identity = jnp.broadcast_to(
        jnp.eye(head_dim, dtype=jnp.float32), (head_count, head_dim, head_dim)
    )
    nothing = jnp.zeros((head_count, head_dim, head_dim), jnp.float32)

    def through(running_pair, block_maps):
        return (compose(running_pair, block_maps), None)

    slab_pair, unused_rest = lax.scan(through, (identity, nothing), (transit, carried))
    slab_transit, slab_state = slab_pair
    scanned = carried_in((slab_transit, slab_state), SEQ, compose, (identity, nothing))
    incoming = scanned[1]

    def advance(carry_state, block_maps):
        following = (
            jnp.einsum("hde,hef->hdf", block_maps[0], carry_state, precision=exact_mode)
            + block_maps[1]
        )
        return (following, carry_state)

    unused_last, starts = lax.scan(advance, incoming, (transit, carried))
    outputs = local_out + jnp.einsum("nhrd,nhde->nhre", reader, starts, precision=exact_mode)
    head_out = outputs.transpose(0, 2, 1, 3).reshape(tokens, head_count, head_dim)
    gate_rows = gate_raw.reshape(tokens, head_count, head_dim)
    scaled = head_out * lax.rsqrt(
        jnp.mean(head_out * head_out, axis=-1, keepdims=True) + norm_floor
    )
    hidden = (
        (scaled * norm_gain * jax.nn.silu(gate_rows))
        .reshape(tokens, head_count * head_dim)
        .astype(jnp.bfloat16)
    )
    column_weight = lax.all_to_all(out_weight, "head", split_axis=1, concat_axis=0, tiled=True)
    summed = jnp.dot(collect(hidden, "head", 1), column_weight, preferred_element_type=jnp.float32)
    return summed.astype(jnp.bfloat16)


def solution(mesh):
    finer = Mesh(
        mesh.devices.reshape(8, 4, 2, mesh.shape["head"]), ("seq_0", "seq_1", "seq_2", "head")
    )
    return jax.shard_map(
        on_device,
        mesh=finer,
        in_specs=(
            P(SEQ, "head"),
            P(None, "head"),
            P(None, "head"),
            P(None, "head"),
            P(None, "head"),
            P(None, "head"),
            P(None, "head"),
            P(None, None, "head"),
            P("head"),
            P("head"),
            P("head"),
            P(),
            P("head", None),
        ),
        out_specs=P(SEQ, "head"),
        check_vma=False,
    )
```

profile of v0, /device:TPU:8, one launch (start us, length us, event | category | flops | bytes accessed | tf_op | source)
XLA Modules:
  0.0 231.8 jit_solution(16035866141420245483)
XLA Ops:
  7.5 1.2 exponential_negate_fusion
  8.7 1.5 fusion.183
  10.7 34.6 %all-gather.10.cloned.1.call-done = bf16[512,2048]{1,0:T(8,128)(2,1)} async-done(((bf16[512,512]{1,0:T(8,128)(2,1)}), bf16[512,2048]{1,0:T(8,128)(2,1)}) %all-gather.10.cloned.1.call-update) | async-done | bytes 2097168 | tf_op jit(solution)/shard_map/all_gather | solution.py:167
  45.4 2.4 %fusion.166 = f32[4,2,128]{2,1,0:T(2,128)S(1)} fusion(bf16[512,2048]{1,0:T(8,128)(2,1)} %all-gather.10.cloned.1.call-done, bf16[2048,2]{0,1:T(2,128)(2,1)} %param.23, f32[2]{0:T(128)} %param.27, f32[2]{0:T(128)} %exponential_negate_fusion), kind=kOutput, calls=%fused_computation.232 | convolution fusion | flops 4202496 | bytes 2109456 | tf_op jit(solution)/shard_map/dot_general | solution.py:169
  47.8 1.2 reduce_window_sum.11
  52.8 2.1 collective-permute-start
  55.7 2.1 collective-permute-done
  57.8 1.9 fusion.182
  61.1 1.4 fusion.17
  70.8 0.9 fusion.65
  71.7 1.5 fusion.193
  73.1 1.1 bitcast_multiply_fusion.3
  74.3 1.6 fusion.181
  76.4 2.2 fusion.26
  78.7 1.3 fusion.79
  80.0 1.3 fusion.80
  81.4 2.4 %while.28 = (s32[]{:T(128)}, f32[2,128,128]{2,1,0:T(8,128)S(1)}, f32[2,128,128]{2,1,0:T(8,128)S(1)}, f32[4,2,128,128]{3,2,1,0:T(8,128)S(1)}, f32[4,2,128,128]{3,2,1,0:T(8,128)S(1)}) while((s32[]{:T(128)}, f32[2,128,128]{2,1,0:T(8,128)S(1)}, f32[2,128,128]{2,1,0:T(8,128)S(1)}, f32[4,2,128,128]{3,2,1,0:T(8,128)S(1)}, ...), condition=%wide.region_4.5_spmd.clone.clone, body=%wide.region_3.4_spmd.clone.sunk.clone | while | flops 100728832 | bytes 1443410 | solution.py:213
  85.2 2.2 all-gather
  88.3 13.5 %all-gather.1 = f32[8,128,128]{2,1,0:T(8,128)S(1)} all-gather(f32[2,128,128]{2,1,0:T(8,128)S(1)} %fusion.195), channel_id=3, replica_groups=mesh['seq_0'=8,'seq_1'=4,'seq_2'=2,'head'=4] {'seq_1'}, dimensions={0}, use_global_device_ids=true | all-gather | bytes 655360 | tf_op jit(solution)/shard_map/all_gather | solution.py:32
  104.6 0.9 fusion.198
  105.6 2.3 copy.83
  107.8 2.3 copy.84
  110.1 4.2 %all-to-all-start.1 = ((bf16[256,4,512]{2,0,1:T(8,128)(2,1)}), bf16[256,4,512]{2,0,1:T(8,128)(2,1)}, u32[]{:S(2)}, u32[]{:S(2)}) async-start(bf16[256,4,512]{2,0,1:T(8,128)(2,1)} %copy.84), calls=%async_computation.1 | async-start | bytes 2097152 | tf_op jit(solution)/shard_map/all_to_all | solution.py:237
  114.4 2.2 all-gather.3
  117.8 13.5 %all-gather.4 = f32[8,128,128]{2,1,0:T(8,128)S(1)} all-gather(f32[2,128,128]{2,1,0:T(8,128)S(1)} %convolution_add_fusion.13), channel_id=6, replica_groups=mesh['seq_0'=8,'seq_1'=4,'seq_2'=2,'head'=4] {'seq_1'}, dimensions={0}, use_global_device_ids=true | all-gather | bytes 655360 | tf_op jit(solution)/shard_map/all_gather | solution.py:32
  133.1 0.9 convolution_add_fusion.10
  134.2 2.2 mul.279
  136.3 2.4 %reduce_sum.27 = f32[512,2]{1,0:T(8,128)} reduce(f32[512,2,128]{2,1,0:T(2,128)} %mul.279, f32[]{:T(128)} %constant.233.clone.1), dimensions={2}, to_apply=%region_1.2 | reduce | flops 130048 | bytes 528388 | tf_op jit(solution)/shard_map/reduce_sum | solution.py:73
  138.7 1.0 add_rsqrt_fusion.1
  139.8 2.2 reshape.130
  142.0 2.5 %fusion.18 = f32[4,2,128,128]{3,2,1,0:T(8,128)S(1)} fusion(f32[4,128,2,128]{3,2,1,0:T(2,128)} %reshape.130, f32[4,128,2,128]{3,2,1,0:T(2,128)S(1)} %copy-done.2, f32[4,128,2]{1,2,0:T(2,128)S(1)} %bitcast.192, f32[4,128,2]{1,2,0:T(2,128)S(1)} %bitcast.193, f32[4,2,128]{2,1,0:T(2,128)S(1)} %reduce_window_sum.11, pred[128,128]{1,0:T(8,128)(4,1)S(1)} %get-tuple-element.135), kind=kOutput, calls=%fused_computation.25 | convolution fusion | flops 202244096 | bytes 1601536 | tf_op jit(solution)/shard_map/...rd,...sd->...rs/dot_general | solution.py:119
  144.5 1.5 fusion.82
  147.0 1.8 fusion.85
  148.8 35.7 %all-gather.14.cloned.1.call-done = f32[16,128,128]{2,1,0:T(8,128)} async-done(((f32[2,128,128]{2,1,0:T(8,128)}), f32[16,128,128]{2,1,0:T(8,128)}) %all-gather.14.cloned.1.call-update) | async-done | bytes 1048592 | tf_op jit(solution)/shard_map/all_gather | solution.py:32
  184.5 1.3 convolution_add_fusion.16
  185.8 1.2 convolution_add_fusion.9
  187.1 1.2 convolution_add_fusion.8
  188.3 1.2 convolution_add_fusion.7
  191.2 7.5 %while.27 = (s32[]{:T(128)}, f32[2,128,128]{2,1,0:T(8,128)S(1)}, f32[4,2,128,128]{3,2,1,0:T(8,128)}, f32[4,2,128,128]{3,2,1,0:T(8,128)S(1)}, f32[4,2,128,128]{3,2,1,0:T(8,128)}) while((s32[]{:T(128)}, f32[2,128,128]{2,1,0:T(8,128)S(1)}, f32[4,2,128,128]{3,2,1,0:T(8,128)}, f32[4,2,128,128]{3,2,1,0:T(8,128)S(1)}, ...), condition=%wide.region_6.7_spmd.clone, body=%wide.region_5.6_spmd.sunk.clone | while | flops 50364416 | bytes 1049673 | solution.py:225
  191.9 1.2 convolution_add_fusion.24
  193.8 1.2 convolution_add_fusion.24
  195.7 1.2 convolution_add_fusion.24
  197.6 1.2 convolution_add_fusion.24
  198.7 3.8 %multiply_reduce_fusion = (f32[4,128,2]{1,2,0:T(2,128)S(1)}, f32[4,128,2,128]{1,3,2,0:T(8,128)}) fusion(f32[4,2,128,128]{2,3,1,0:T(8,128)} %fusion.85, f32[4,2,128,128]{3,2,1,0:T(8,128)} %get-tuple-element.62, f32[4,2,128,128]{3,2,1,0:T(8,128)} %fusion.82, f32[4,128,2,128]{3,2,1,0:T(2,128)} %reshape.130, f32[4,2,128]{2,1,0:T(2,128)S(1)} %get-tuple-element.120, ...), kind=kOutput, calls=%fused_computation.103 | convolution fusion | flops 202112000 | bytes 2633728 | tf_op jit(solution)/shard_map/nhrd,nhde->nhre/dot_general | solution.py:226
  202.7 2.0 copy.81
  205.4 2.1 fusion.55
  207.6 14.9 %all_to_all.21 = bf16[4,512,256]{2,1,0:T(8,128)(2,1)S(1)} all-to-all(bf16[4,512,256]{2,1,0:T(8,128)(2,1)S(1)} %broadcast_in_dim.110), channel_id=1, replica_groups=mesh['seq_0'=8,'seq_1'=4,'seq_2'=2,'head'=4] {'head'}, dimensions={0} | all-to-all | bytes 2097152 | tf_op jit(solution)/shard_map/all_to_all | solution.py:44
  222.5 2.7 %fusion.14 = bf16[512,512]{1,0:T(8,128)(2,1)} fusion(bf16[256,4,512]{2,0,1:T(8,128)(2,1)} %all-to-all-done.1, bf16[4,512,256]{2,1,0:T(8,128)(2,1)S(1)} %all_to_all.21), kind=kOutput, calls=%fused_computation.18 | convolution fusion | flops 537133056 | bytes 2621440 | tf_op jit(solution)/shard_map/dot_general | solution.py:238
  (216 shorter events, 32.3 us)
Async XLA Ops:
  6.5 42.8 %copy-start = (bf16[2048,256]{1,0:T(8,128)(2,1)S(1)}, bf16[2048,256]{1,0:T(8,128)(2,1)}, u32[]{:S(2)}) copy-start(bf16[2048,256]{1,0:T(8,128)(2,1)} %param.20) | copy-start | bytes 3145732
  6.5 38.8 %all-gather.10.cloned.1.call-start = ((), (), s32[]{:S(2)}) async-start(), calls=%async_computation.2 | async-start | bytes 2621440 | tf_op jit(solution)/shard_map/all_gather | solution.py:167
  7.3 141.5 %all-gather.12.cloned.1.call-start = ((), (), s32[]{:S(2)}) async-start(), calls=%async_computation.3 | async-start | bytes 1179648 | tf_op jit(solution)/shard_map/all_gather | solution.py:32
  45.4 3.9 %copy-start.5 = (bf16[512,2048]{1,0:T(8,128)(2,1)S(1)}, bf16[512,2048]{1,0:T(8,128)(2,1)}, u32[]{:S(2)}) copy-start(bf16[512,2048]{1,0:T(8,128)(2,1)} %all-gather.10.cloned.1.call-done) | copy-start | bytes 6291460
  49.3 1.2 copy-start.48
  50.0 2.8 %copy-start.34 = (f32[512,256]{1,0:T(8,128)}, f32[512,256]{1,0:T(8,128)S(1)}, u32[]{:S(2)}) copy-start(f32[512,256]{1,0:T(8,128)S(1)} %fusion.188) | copy-start | bytes 1572868
  50.0 2.0 copy-start.49
  51.2 0.8 copy-start.38
  52.0 2.9 %copy-start.39 = (bf16[2048,2]{0,1:T(2,128)(2,1)S(1)}, bf16[2048,2]{0,1:T(2,128)(2,1)}, u32[]{:S(2)}) copy-start(bf16[2048,2]{0,1:T(2,128)(2,1)} %param.22) | copy-start | bytes 24580
  52.0 2.9 %copy-start.47 = (f32[2]{0:T(128)S(1)}, f32[2]{0:T(128)}, u32[]{:S(2)}) copy-start(f32[2]{0:T(128)} %param.26) | copy-start | bytes 28
  52.8 2.8 %copy-start.36 = (f32[512,256]{1,0:T(8,128)}, f32[512,256]{1,0:T(8,128)S(1)}, u32[]{:S(2)}) copy-start(f32[512,256]{1,0:T(8,128)S(1)} %fusion.186) | copy-start | bytes 1572868
  52.8 5.0 %collective-permute-start = (f32[3,768]{1,0:T(4,128)S(1)}, f32[3,768]{1,0:T(4,128)S(1)}, u32[]{:S(2)}, u32[]{:S(2)}) collective-permute-start(f32[3,768]{1,0:T(4,128)S(1)} %pad_maximum_fusion.3), channel_id=1, source_target_pairs={{0,4},{4,8},{8,12},{12,16},{16,20},{20,24},{24,28},{28,32},{32,36}... | collective-permute-start | bytes 27656 | tf_op jit(solution)/shard_map/ppermute | solution.py:18
  61.1 18.9 %copy-start.1 = (f32[4,128,2,128]{3,2,1,0:T(2,128)}, f32[4,128,2,128]{3,2,1,0:T(2,128)S(1)}, u32[]{:S(2)}) copy-start(f32[4,128,2,128]{3,2,1,0:T(2,128)S(1)} %reshape.131) | copy-start | bytes 1572868
  70.7 3.6 %copy-start.3 = (f32[4,2,128,128]{3,2,1,0:T(8,128)}, f32[4,2,128,128]{3,2,1,0:T(8,128)S(1)}, u32[]{:S(2)}) copy-start(f32[4,2,128,128]{3,2,1,0:T(8,128)S(1)} %sub.166) | copy-start | bytes 1572868
  70.7 3.6 %copy-start.35 = (f32[512,256]{1,0:T(8,128)S(1)}, f32[512,256]{1,0:T(8,128)}, u32[]{:S(2)}) copy-start(f32[512,256]{1,0:T(8,128)} %copy-done.34) | copy-start | bytes 1572868
  70.7 3.6 %copy-start.37 = (f32[512,256]{1,0:T(8,128)S(1)}, f32[512,256]{1,0:T(8,128)}, u32[]{:S(2)}) copy-start(f32[512,256]{1,0:T(8,128)} %copy-done.36) | copy-start | bytes 1572868
  70.7 3.6 %copy-start.40 = (f32[1,1,256]{2,0,1:T(1,128)S(1)}, f32[1,1,256]{2,0,1:T(1,128)}, u32[]{:S(2)}) copy-start(f32[1,1,256]{2,0,1:T(1,128)} %get-tuple-element.106) | copy-start | bytes 3076
  70.7 3.6 %copy-start.41 = (f32[1,1,256]{2,0,1:T(1,128)S(1)}, f32[1,1,256]{2,0,1:T(1,128)}, u32[]{:S(2)}) copy-start(f32[1,1,256]{2,0,1:T(1,128)} %get-tuple-element.111) | copy-start | bytes 3076
  70.7 3.6 %copy-start.42 = (f32[1,1,256]{2,0,1:T(1,128)S(1)}, f32[1,1,256]{2,0,1:T(1,128)}, u32[]{:S(2)}) copy-start(f32[1,1,256]{2,0,1:T(1,128)} %get-tuple-element.112) | copy-start | bytes 3076
  70.7 3.6 %copy-start.43 = (f32[1,1,256]{2,0,1:T(1,128)S(1)}, f32[1,1,256]{2,0,1:T(1,128)}, u32[]{:S(2)}) copy-start(f32[1,1,256]{2,0,1:T(1,128)} %get-tuple-element.113) | copy-start | bytes 3076
  70.7 3.6 %copy-start.44 = (f32[1,1,256]{2,0,1:T(1,128)S(1)}, f32[1,1,256]{2,0,1:T(1,128)}, u32[]{:S(2)}) copy-start(f32[1,1,256]{2,0,1:T(1,128)} %get-tuple-element.114) | copy-start | bytes 3076
  70.7 3.6 %copy-start.45 = (f32[1,1,256]{2,0,1:T(1,128)S(1)}, f32[1,1,256]{2,0,1:T(1,128)}, u32[]{:S(2)}) copy-start(f32[1,1,256]{2,0,1:T(1,128)} %get-tuple-element.115) | copy-start | bytes 3076
  70.8 3.6 %copy-start.46 = (f32[1,1,256]{2,0,1:T(1,128)S(1)}, f32[1,1,256]{2,0,1:T(1,128)}, u32[]{:S(2)}) copy-start(f32[1,1,256]{2,0,1:T(1,128)} %get-tuple-element.116) | copy-start | bytes 3076
  74.3 2.1 copy-start.4
  85.2 2.5 %copy-start.8 = (f32[4,2,128,128]{3,2,1,0:T(8,128)}, f32[4,2,128,128]{3,2,1,0:T(8,128)S(1)}, u32[]{:S(2)}) copy-start(f32[4,2,128,128]{3,2,1,0:T(8,128)S(1)} %get-tuple-element.279) | copy-start | bytes 1572868
  87.6 0.7 copy-start.15
  88.3 13.5 %copy-start.17 = (f32[2,128,128]{2,1,0:T(8,128)}, f32[2,128,128]{2,1,0:T(8,128)S(1)}, u32[]{:S(2)}) copy-start(f32[2,128,128]{2,1,0:T(8,128)S(1)} %fusion.195) | copy-start | bytes 393220
  102.1 0.7 copy-start.21
  110.1 97.4 %all-to-all-start.1 = ((bf16[256,4,512]{2,0,1:T(8,128)(2,1)}), bf16[256,4,512]{2,0,1:T(8,128)(2,1)}, u32[]{:S(2)}, u32[]{:S(2)}) async-start(bf16[256,4,512]{2,0,1:T(8,128)(2,1)} %copy.84), calls=%async_computation.1 | async-start | bytes 2097152 | tf_op jit(solution)/shard_map/all_to_all | solution.py:237
  114.4 70.2 %all-gather.14.cloned.1.call-start = ((), (), s32[]{:S(2)}) async-start(), calls=%async_computation.4 | async-start | bytes 1179648 | tf_op jit(solution)/shard_map/all_gather | solution.py:32
  117.5 16.6 %copy-start.50 = (f32[128]{0:T(128)S(1)}, f32[128]{0:T(128)}, u32[]{:S(2)}) copy-start(f32[128]{0:T(128)} %param.28) | copy-start | bytes 1540
  117.8 14.3 %copy-start.11 = (f32[2,128,128]{2,1,0:T(8,128)}, f32[2,128,128]{2,1,0:T(8,128)S(1)}, u32[]{:S(2)}) copy-start(f32[2,128,128]{2,1,0:T(8,128)S(1)} %convolution_add_fusion.13) | copy-start | bytes 393220
  134.1 7.9 %copy-start.2 = (f32[4,128,2,128]{3,2,1,0:T(2,128)S(1)}, f32[4,128,2,128]{3,2,1,0:T(2,128)}, u32[]{:S(2)}) copy-start(f32[4,128,2,128]{3,2,1,0:T(2,128)} %copy-done.1) | copy-start | bytes 1572868
  139.8 6.2 %copy-start.16 = (f32[2,128,128]{2,1,0:T(8,128)S(1)}, f32[2,128,128]{2,1,0:T(8,128)}, u32[]{:S(2)}) copy-start(f32[2,128,128]{2,1,0:T(8,128)} %copy-done.15) | copy-start | bytes 393220
  139.8 6.2 %copy-start.18 = (f32[2,128,128]{2,1,0:T(8,128)S(1)}, f32[2,128,128]{2,1,0:T(8,128)}, u32[]{:S(2)}) copy-start(f32[2,128,128]{2,1,0:T(8,128)} %copy-done.17) | copy-start | bytes 393220
  142.0 4.3 %copy-start.20 = (f32[2,128,128]{2,1,0:T(8,128)S(1)}, f32[2,128,128]{2,1,0:T(8,128)}, u32[]{:S(2)}) copy-start(f32[2,128,128]{2,1,0:T(8,128)} %convolution_add_fusion.10) | copy-start | bytes 393220
  142.0 4.4 %copy-start.28 = (f32[2,128,128]{2,1,0:T(8,128)S(1)}, f32[2,128,128]{2,1,0:T(8,128)}, u32[]{:S(2)}) copy-start(f32[2,128,128]{2,1,0:T(8,128)} %copy-done.27) | copy-start | bytes 393220
  142.0 4.4 %copy-start.30 = (f32[2,128,128]{2,1,0:T(8,128)S(1)}, f32[2,128,128]{2,1,0:T(8,128)}, u32[]{:S(2)}) copy-start(f32[2,128,128]{2,1,0:T(8,128)} %copy-done.29) | copy-start | bytes 393220
  142.0 4.4 %copy-start.32 = (f32[2,128,128]{2,1,0:T(8,128)S(1)}, f32[2,128,128]{2,1,0:T(8,128)}, u32[]{:S(2)}) copy-start(f32[2,128,128]{2,1,0:T(8,128)} %copy-done.31) | copy-start | bytes 393220
  142.0 4.7 %copy-start.19 = (f32[2,128,128]{2,1,0:T(8,128)S(1)}, f32[2,128,128]{2,1,0:T(8,128)}, u32[]{:S(2)}) copy-start(f32[2,128,128]{2,1,0:T(8,128)} %fusion.198) | copy-start | bytes 393220
  142.0 4.7 %copy-start.22 = (f32[2,128,128]{2,1,0:T(8,128)S(1)}, f32[2,128,128]{2,1,0:T(8,128)}, u32[]{:S(2)}) copy-start(f32[2,128,128]{2,1,0:T(8,128)} %copy-done.21) | copy-start | bytes 393220
  142.0 4.7 %copy-start.24 = (f32[2,128,128]{2,1,0:T(8,128)S(1)}, f32[2,128,128]{2,1,0:T(8,128)}, u32[]{:S(2)}) copy-start(f32[2,128,128]{2,1,0:T(8,128)} %copy-done.23) | copy-start | bytes 393220
  142.0 4.7 %copy-start.26 = (f32[2,128,128]{2,1,0:T(8,128)S(1)}, f32[2,128,128]{2,1,0:T(8,128)}, u32[]{:S(2)}) copy-start(f32[2,128,128]{2,1,0:T(8,128)} %copy-done.25) | copy-start | bytes 393220
  148.8 39.5 %copy-start.7 = (f32[16,128,128]{2,1,0:T(8,128)S(1)}, f32[16,128,128]{2,1,0:T(8,128)}, u32[]{:S(2)}) copy-start(f32[16,128,128]{2,1,0:T(8,128)} %all-gather.12.cloned.1.call-done) | copy-start | bytes 3145732
  184.5 5.0 %copy-start.33 = (f32[16,128,128]{2,1,0:T(8,128)S(1)}, f32[16,128,128]{2,1,0:T(8,128)}, u32[]{:S(2)}) copy-start(f32[16,128,128]{2,1,0:T(8,128)} %all-gather.14.cloned.1.call-done) | copy-start | bytes 3145732
  189.5 1.4 copy-start.12
  189.5 1.4 copy-start.14
  198.7 6.7 %copy-start.6 = (bf16[512,2048]{1,0:T(8,128)(2,1)S(1)}, bf16[512,2048]{1,0:T(8,128)(2,1)}, u32[]{:S(2)}) copy-start(bf16[512,2048]{1,0:T(8,128)(2,1)} %all-gather.10.cloned.1.call-done) | copy-start | bytes 6291460
  (8 other events, 5.2 us)
Sparse Core Ops, SparseCore 0:
  9.1 36.1 all-gather.9
  105.7 40.1 all-gather.11
  147.7 36.7 all-gather.13
where the time goes:
time: 233 us; the launch traced here: 232 us
  waiting for transfers between devices  73.2 us (31%)
  matrix products  54.7 us (23%)
  blocking collectives  46.3 us (20%)
  local copies, waits for them, and re-layouts  24.2 us (10%)
  between operations  14.3 us (6%)
  other arithmetic  12.4 us (5%)
  starting transfers between devices  6.43 us (3%)
    all_gather x2, waiting for transfers between devices, carried_in(): pieces = jax.tree.map(lambda part: lax.all_gather(part, axis), subtotal)  35.7 us
    all_gather x1, waiting for transfers between devices, on_device(): shard_piece = lax.all_gather(layer_in, 'head', axis=1, tiled=True)  34.6 us
    all_gather x4, blocking collectives, carried_in(): pieces = jax.tree.map(lambda part: lax.all_gather(part, axis), subtotal)  31.4 us
    all_to_all x1, blocking collectives, copy_for_each(): lax.all_to_all(jnp.broadcast_to(value[None], (length, *value.shape)), axi...  14.9 us
    dot_general x21, matrix products, compose(): jnp.einsum('...de,...ef->...df', later_map[0], earlier[1], precision=exac...  10.1 us
    unnamed x105, local copies, waits for them, and re-layouts  9.2 us
    dot_general x6, matrix products, on_device(): jnp.dot(shard_piece, weight, preferred_element_type=jnp.float32)  7.33 us
    dot_general x7, matrix products, unit_lower_inverse(): jnp.einsum('...rs,...st->...rt', inverse, middle, precision=exact_mode)  5.3 us
  transfers between devices with their start and end apart: 5, of which 3 were waited for; matrix products, arithmetic and copies ran while one was open for 21% of the time, Pallas kernels for 0%

commit v1 on v0

v1 whole, which is shorter than its diff:
```python
import functools

import jax
import jax.numpy as jnp
from jax import lax
from jax.experimental import pallas as pl
from jax.experimental.pallas import tpu as pltpu
from jax.sharding import Mesh
from jax.sharding import PartitionSpec as P

F32 = jnp.float32
BF16 = jnp.bfloat16
MESH = pl.DeviceIdType.MESH
SEQ = ("z", "y", "c")
BLK = 128
HALF = BLK // 2
PRE = 16
NORM_FLOOR = 0.0001

NN = (((1,), (0,)), ((), ()))


def dot1(a, b):
    return lax.dot_general(a, b, NN, preferred_element_type=F32)


def halves(a):
    hi = a.astype(BF16)
    lo = (a - hi.astype(F32)).astype(BF16)
    return hi, lo


def left3(a):
    hi, lo = halves(a)
    return jnp.concatenate([hi, hi, lo], axis=1)


def right3(b):
    hi, lo = halves(b)
    return jnp.concatenate([hi, lo, hi], axis=0)


def dot3(a, b):
    return dot1(left3(a), right3(b))


def dot_exact_left(a_bf16, b):
    hi, lo = halves(b)
    return dot1(
        jnp.concatenate([a_bf16, a_bf16], axis=1), jnp.concatenate([hi, lo], axis=0)
    )


def sigmoid(v):
    return 1.0 / (1.0 + jnp.exp(-v))


def silu(v):
    return v / (1.0 + jnp.exp(-v))


def softplus(v):
    return jnp.maximum(v, 0.0) + jnp.log(1.0 + jnp.exp(-jnp.abs(v)))


def compose(later, earlier):
    l2, b2, c2 = later
    l1, b1, c1 = earlier
    moved = dot3(l2, jnp.concatenate([l1, b1], axis=1))
    width = l1.shape[1]
    return (
        c2[:, :width] * l1 + c1[:, :width] * l2 - moved[:, :width],
        c2[:, :width] * b1 + b2 - moved[:, width:],
        c1 * c2,
    )


def apply_map(m, state):
    l, b, c = m
    return c[:, : state.shape[1]] * state - dot3(l, state) + b


def pick(flag, m, other):
    return jax.tree.map(lambda a, b: jnp.where(flag, a, b), m, other)


def kernel(
    sizes,
    x_in,
    wq,
    wk,
    wv,
    wg,
    wbd,
    conv_w,
    decay_log,
    beta_bias,
    decay_bias,
    norm_gain,
    w_out,
    out,
    xg,
    w_all,
    col_w,
    state,
    logsum,
    prelim,
    gate,
    hg,
    sc_send,
    sc_recv,
    yb,
    zb,
    fin_send,
    sin,
    load_sem,
    pre_send,
    pre_recv,
    d_send,
    d_recv,
    f_send,
    f_recv,
    w_send,
    w_recv,
    c_send,
    c_recv,
    y_send,
    y_recv,
    z_send,
    z_recv,
    hd_send,
    hd_recv,
    hf_send,
    hf_recv,
):
    nz, ny, nx = sizes["z"], sizes["y"], sizes["x"]
    z = lax.axis_index("z")
    y = lax.axis_index("y")
    c = lax.axis_index("c")
    x = lax.axis_index("x")
    tokens = x_in.shape[0]
    feats = x_in.shape[1]
    chunks = tokens // BLK
    heads = 2
    width = heads * BLK
    right, left = lax.rem(x + 1, nx), lax.rem(x + nx - 1, nx)
    far = lax.rem(x + 2, nx)
    count = nz * ny * 2
    here = (z * ny + y) * 2 + c
    after = lax.rem(here + 1, count)
    prior = lax.rem(here + count - 1, count)

    def place(s, xx):
        return {"z": s // (ny * 2), "y": lax.rem(s // 2, ny), "c": lax.rem(s, 2), "x": xx}

    weights = (wq, wk, wv, wg)
    loads = [pltpu.make_async_copy(x_in, xg.at[x, pl.ds(PRE, tokens), :], load_sem.at[0])]
    loads[0].start()
    for i, w in enumerate(weights):
        cp = pltpu.make_async_copy(
            w, w_all.at[:, pl.ds(i * width, width)], load_sem.at[1 + i]
        )
        cp.start()
        loads.append(cp)
    cp = pltpu.make_async_copy(wbd, w_all.at[:, pl.ds(4 * width, BLK)], load_sem.at[5])
    cp.start()
    loads.append(cp)
    own_cols = pltpu.make_async_copy(
        w_out.at[:, pl.ds(pl.multiple_of(x * feats, feats), feats)],
        col_w.at[pl.ds(pl.multiple_of(x * width, width), width), :],
        load_sem.at[6],
    )
    own_cols.start()

    barrier = pltpu.get_barrier_semaphore()
    up_y, down_y = lax.rem(y + 1, ny), lax.rem(y + ny - 1, ny)
    up_z, down_z = lax.rem(z + 1, nz), lax.rem(z + nz - 1, nz)
    partners = [{"x": right}, {"x": left}, {"x": far}, {"c": 1 - c}]
    partners += [{"y": up_y}, {"y": down_y}, {"z": up_z}, {"z": down_z}]
    partners += [place(after, i) for i in range(nx)]
    partners += [place(prior, i) for i in range(nx)]
    for who in partners:
        pl.semaphore_signal(barrier, inc=1, device_id=who, device_id_type=MESH)

    state[...] = jnp.zeros_like(state)
    eye = (
        lax.broadcasted_iota(jnp.int32, (BLK, BLK), 0)
        == lax.broadcasted_iota(jnp.int32, (BLK, BLK), 1)
    ).astype(F32)
    for h in range(heads):
        state[h, :, 0:BLK] = eye
    logsum[...] = jnp.zeros_like(logsum)
    pl.semaphore_wait(barrier, len(partners))
    loads[0].wait()

    def remote(src, dst, send, recv, who):
        return pltpu.make_async_remote_copy(
            src_ref=src,
            dst_ref=dst,
            send_sem=send,
            recv_sem=recv,
            device_id=who,
            device_id_type=MESH,
        )


    def ring(buf, base, send, recv, relay_send, relay_recv):
        def direct(way, t):
            rows = pl.ds(pl.multiple_of(base + t * BLK, PRE), BLK)
            return remote(
                buf.at[x, rows, :],
                buf.at[x, rows, :],
                send.at[way, t],
                recv.at[way, t],
                {"x": (right, left)[way]},
            )

        def relay(way, t):
            rows = pl.ds(pl.multiple_of(base + t * BLK + way * HALF, PRE), HALF)
            source = (left, right)[way]
            return remote(
                buf.at[source, rows, :],
                buf.at[source, rows, :],
                relay_send.at[way, t],
                relay_recv.at[way, t],
                {"x": (right, left)[way]},
            )

        return direct, relay

    direct, relay = ring(xg, PRE, d_send, d_recv, f_send, f_recv)

    def pre_copy(i):
        return remote(
            xg.at[x, pl.ds(tokens, PRE), :],
            xg.at[x, pl.ds(0, PRE), :],
            pre_send.at[i],
            pre_recv.at[x],
            place(after, i),
        )

    for i in range(nx):
        pre_copy(i).start()
    for t in range(2):
        for way in range(2):
            direct(way, t).start()
    for cp in loads[1:]:
        cp.wait()

    row_i = lax.broadcasted_iota(jnp.int32, (BLK, BLK), 0)
    col_i = lax.broadcasted_iota(jnp.int32, (BLK, BLK), 1)
    differ = jnp.bitwise_xor(row_i, col_i)
    within = row_i >= col_i
    before = row_i > col_i

    lane = lax.broadcasted_iota(jnp.int32, (1, BLK), 1)
    bias_row = jnp.where(lane == 0, beta_bias[0], 0.0)
    bias_row = jnp.where(lane == 1, beta_bias[1], bias_row)
    bias_row = jnp.where(lane == 2, decay_bias[0], bias_row)
    bias_row = jnp.where(lane == 3, decay_bias[1], bias_row)
    rate_row = jnp.where(lane == 2, decay_log[0], -200.0)
    rate_row = jnp.exp(jnp.where(lane == 3, decay_log[1], rate_row))
    gain_row = norm_gain[...].reshape(1, BLK)

    def unit_rows(v):
        return v * lax.rsqrt(jnp.sum(v * v, axis=-1, keepdims=True) + 1.0)

    def chunk(t):
        start = pl.multiple_of(t * BLK, BLK)
        rows = pl.ds(start, BLK + PRE)
        xs = jnp.concatenate([xg[p, rows, :] for p in range(nx)], axis=1)
        first = jnp.logical_and(here == 0, t == 0)
        ext_row = lax.broadcasted_iota(jnp.int32, (BLK + PRE, 3 * width), 0)
        raw = dot1(xs, w_all[...])
        qkv = raw[:, 0 : 3 * width]
        qkv = jnp.where(jnp.logical_and(first, ext_row < PRE), 0.0, qkv)
        taps = [
            jnp.concatenate([conv_w[s, i : i + 1, :] for i in range(3)], axis=1)
            for s in range(4)
        ]
        mixed = taps[0] * qkv
        for s in range(1, 4):
            mixed = mixed + taps[s] * pltpu.roll(qkv, s, 0)
        mixed = silu(mixed[PRE:])
        out_rows = pl.ds(start, BLK)
        gates = silu(raw[PRE:, 3 * width : 4 * width])
        for h in range(heads):
            gate[out_rows, h * BLK : (h + 1) * BLK] = (
                gates[:, h * BLK : (h + 1) * BLK] * gain_row
            )
        small = raw[PRE:, 4 * width :] + bias_row
        betas = sigmoid(small)
        steps = -rate_row * softplus(small)
        s_hi = steps.astype(BF16)
        rest = steps - s_hi.astype(F32)
        s_mid = rest.astype(BF16)
        s_lo = (rest - s_mid.astype(F32)).astype(BF16)
        tri = within.astype(F32).astype(BF16)
        total = dot1(
            jnp.concatenate([tri, tri, tri], axis=1),
            jnp.concatenate([s_hi, s_mid, s_lo], axis=0),
        )
        total_t = jnp.transpose(total)
        both = []
        for h in range(heads):
            cols = slice(h * BLK, (h + 1) * BLK)
            q = unit_rows(mixed[:, h * BLK : (h + 1) * BLK])
            k = unit_rows(mixed[:, width + h * BLK : width + (h + 1) * BLK])
            v = mixed[:, 2 * width + h * BLK : 2 * width + (h + 1) * BLK]
            beta = betas[:, h : h + 1]
            run_c = total[:, 2 + h : 3 + h]
            run_r = total_t[2 + h : 3 + h, :]
            end = run_r[:, BLK - 1 : BLK]
            decay = jnp.where(within, jnp.exp(jnp.minimum(run_c - run_r, 0.0)), 0.0)
            kt = jnp.transpose(k)
            scores = dot3(jnp.concatenate([k, q], axis=0), kt)
            low = jnp.where(before, beta * decay * scores[:BLK], 0.0)
            mix = decay * scores[BLK:]
            grow = jnp.exp(run_c)
            ext = state[h]
            read = dot3(
                jnp.concatenate([(beta * grow) * k, grow * q], axis=0), ext
            )
            right_side = (
                jnp.concatenate([jnp.zeros_like(v), beta * v], axis=1) - read[:BLK]
            )
            both.append((low, mix, right_side, read[BLK:], kt, run_r, end, ext))
        inv = [
            jnp.where(row_i == col_i, 1.0, 0.0) - jnp.where(differ == 1, b[0], 0.0)
            for b in both
        ]
        w = 2
        while w < BLK:
            linking = jnp.logical_and(differ >= w, differ < 2 * w)
            inv3 = [right3(a) for a in inv]
            mids = [
                dot1(left3(jnp.where(linking, b[0], 0.0)), a)
                for b, a in zip(both, inv3)
            ]
            inv = [a - dot3(a, m) for a, m in zip(inv, mids)]
            w *= 2
        for h in range(heads):
            low, mix, right_side, carried, kt, run_r, end, ext = both[h]
            solved = dot3(inv[h], right_side)
            solved3 = right3(solved)
            prelim[h, out_rows, :] = carried + dot1(left3(mix), solved3)
            weighted = kt * jnp.exp(end - run_r)
            state[h] = jnp.exp(end) * ext + dot1(left3(weighted), solved3)
            logsum[h] = logsum[h] + jnp.broadcast_to(end, logsum.shape[1:])

    def step(t, carry):
        @pl.when(t < chunks)
        def _():
            direct(0, t).wait_recv()
            direct(1, t).wait_recv()
            relay(0, t).start()
            relay(1, t).start()

        @pl.when(t < chunks - 2)
        def _():
            direct(0, t + 2).start()
            direct(1, t + 2).start()

        @pl.when(t == 0)
        def _():
            for i in range(nx):
                remote(
                    xg.at[i, pl.ds(tokens, PRE), :],
                    xg.at[i, pl.ds(0, PRE), :],
                    pre_send.at[i],
                    pre_recv.at[i],
                    place(after, i),
                ).wait_recv()

        @pl.when(t > 0)
        def _():
            relay(0, t - 1).wait_recv()
            relay(1, t - 1).wait_recv()
            chunk(t - 1)

        return carry

    lax.fori_loop(0, chunks + 1, step, 0)

    def columns(j):
        who = lax.rem(x + j, nx)
        return remote(
            w_out.at[:, pl.ds(pl.multiple_of(who * feats, feats), feats)],
            col_w.at[pl.ds(pl.multiple_of(x * width, width), width), :],
            w_send.at[j - 1],
            w_recv.at[j - 1],
            {"x": who},
        )

    for j in range(1, nx):
        columns(j).start()

    def own_map(h):
        ext = state[h]
        keep = jnp.exp(logsum[h, 0:1, :])
        return (keep[:, :BLK] * eye - ext[:, :BLK], ext[:, BLK:], keep)

    sl, sb, skeep = own_map(1 - c)
    sc_send[0:BLK, 0:BLK] = sl
    sc_send[0:BLK, BLK:] = sb
    sc_send[BLK:, :] = jnp.broadcast_to(skeep, (8, 2 * BLK))
    swap = remote(sc_send, sc_recv, c_send.at[0], c_recv.at[0], {"c": 1 - c})
    swap.start()
    mine = own_map(c)
    swap.wait()
    other = (sc_recv[0:BLK, 0:BLK], sc_recv[0:BLK, BLK:], sc_recv[BLK : BLK + 1, :])
    is_first = c == 0
    map0 = pick(is_first, mine, other)
    map1 = pick(is_first, other, mine)
    chip_map = compose(map1, map0)

    def put(buf, slot, m):
        l, b, keep = m
        buf[slot, 0:BLK, 0:BLK] = l.astype(BF16)
        buf[slot, 0:BLK, BLK:] = b.astype(BF16)
        hi, lo = halves(keep)
        tail = lax.broadcasted_iota(jnp.int32, (PRE, 2 * BLK), 0)
        buf[slot, BLK:, :] = jnp.where(
            tail == 0, jnp.broadcast_to(hi.astype(F32), (PRE, 2 * BLK)),
            jnp.broadcast_to(lo.astype(F32), (PRE, 2 * BLK)),
        ).astype(BF16)

    def get(buf, slot):
        tail = buf[slot, BLK:, :].astype(F32)
        return (
            buf[slot, 0:BLK, 0:BLK].astype(F32),
            buf[slot, 0:BLK, BLK:].astype(F32),
            tail[0:1] + tail[1:2],
        )

    put(yb, y, chip_map)

    def y_copy(slot, j, who):
        return remote(yb.at[slot], yb.at[slot], y_send.at[j], y_recv.at[j], {"y": who})

    y1 = y_copy(y, 0, up_y)
    y2 = y_copy(y, 1, down_y)
    y1.start()
    y2.start()
    y1.wait_recv()
    y3 = y_copy(down_y, 2, up_y)
    y3.start()
    y2.wait_recv()
    y3.wait_recv()
    zero = jnp.zeros((BLK, BLK), F32)
    one_row = jnp.ones((1, 2 * BLK), F32)
    identity = (zero, zero, one_row)
    maps = [get(yb, j) for j in range(ny)]
    run = maps[0]
    before_row = pick(y == 0, identity, run)
    for j in range(1, ny):
        before_row = pick(y == j, run, before_row) if j > 1 else before_row
        run = compose(maps[j], run)

    put(zb, z, run)

    def z_copy(slot, j, who):
        return remote(zb.at[slot], zb.at[slot], z_send.at[j], z_recv.at[j], {"z": who})

    ups, downs = nz // 2, nz - 1 - nz // 2
    near = identity
    low_state = zero
    flights = []
    for j in range(ups):
        cp = z_copy(lax.rem(z + nz - j, nz), j, up_z)
        cp.start()
        flights.append(cp)
        dn = None
        if j < downs:
            dn = z_copy(lax.rem(z + j, nz), ups + j, down_z)
            dn.start()
            flights.append(dn)
        if j > 0:
            got = pick(z - j >= 0, get(zb, lax.rem(z + nz - j, nz)), identity)
            near = compose(near, got)
            if j <= downs:
                got = pick(z + j - nz >= 0, get(zb, lax.rem(z + j, nz)), identity)
                low_state = apply_map(got, low_state)
        cp.wait_recv()
        if dn is not None:
            dn.wait_recv()
    got = pick(z - ups >= 0, get(zb, lax.rem(z + nz - ups, nz)), identity)
    row_state = apply_map(near, apply_map(got, low_state))
    chip_state = apply_map(before_row, row_state)
    later_state = apply_map(map0, chip_state)
    sin[c] = jnp.where(is_first, chip_state, later_state)
    fin_send[...] = jnp.where(is_first, later_state, chip_state)
    give = remote(fin_send, sin.at[c], c_send.at[1], c_recv.at[1], {"c": 1 - c})
    give.start()
    give.wait()

    h_direct, h_relay = ring(hg, 0, hd_send, hd_recv, hf_send, hf_recv)
    starts = [right3(sin[h]) for h in range(heads)]
    for t in range(chunks):
        rows = slice(t * BLK, (t + 1) * BLK)
        for h in range(heads):
            part = prelim[h, rows, :]
            head_out = dot1(left3(part[:, :BLK]), starts[h]) + part[:, BLK:]
            scaled = head_out * lax.rsqrt(
                jnp.mean(head_out * head_out, axis=-1, keepdims=True) + NORM_FLOOR
            )
            cols = slice(h * BLK, (h + 1) * BLK)
            hg[x, rows, cols] = (scaled * gate[rows, cols]).astype(BF16)
        for way in range(2):
            h_direct(way, t).start()
    for t in range(chunks):
        for way in range(2):
            h_direct(way, t).wait_recv()
            h_relay(way, t).start()
    own_cols.wait()
    for j in range(1, nx):
        columns(j).wait_recv()
    for t in range(chunks):
        rows = slice(t * BLK, (t + 1) * BLK)
        for way in range(2):
            h_relay(way, t).wait_recv()
        rows_all = jnp.concatenate([hg[p, rows, :] for p in range(nx)], axis=1)
        out[rows, :] = dot1(rows_all, col_w[...]).astype(BF16)

    for i in range(nx):
        pre_copy(i).wait_send()
    for t in range(chunks):
        for way in range(2):
            direct(way, t).wait_send()
            relay(way, t).wait_send()
            h_direct(way, t).wait_send()
            h_relay(way, t).wait_send()
    for j in range(1, nx):
        columns(j).wait_send()
    for cp in (y1, y2, y3):
        cp.wait_send()
    for cp in flights:
        cp.wait_send()


def on_device(
    sizes,
    layer_in,
    query_weight,
    key_weight,
    value_weight,
    gate_weight,
    beta_weight,
    decay_weight,
    conv_weight,
    decay_log,
    beta_bias,
    decay_bias,
    norm_gain,
    out_weight,
):
    tokens, feats = layer_in.shape
    depth, width = query_weight.shape
    nz, ny, nx = sizes["z"], sizes["y"], sizes["x"]
    chunks = tokens // BLK
    heads = 2
    small = jnp.concatenate(
        [
            beta_weight,
            decay_weight,
            jnp.zeros((depth, BLK - 2 * heads), BF16),
        ],
        axis=1,
    )
    anyspace = pl.BlockSpec(memory_space=pl.ANY)
    vmem = pl.BlockSpec(memory_space=pltpu.VMEM)
    smem = pl.BlockSpec(memory_space=pltpu.SMEM)
    dma = pltpu.SemaphoreType.DMA
    zc = nz - 1
    return pl.pallas_call(
        functools.partial(kernel, sizes),
        out_shape=jax.ShapeDtypeStruct((tokens, feats), BF16),
        in_specs=[anyspace] * 6 + [vmem] + [smem] * 3 + [vmem, anyspace],
        out_specs=vmem,
        scratch_shapes=[
            pltpu.VMEM((nx, tokens + PRE, feats), BF16),
            pltpu.VMEM((depth, 4 * width + BLK), BF16),
            pltpu.VMEM((nx * width, feats), BF16),
            pltpu.VMEM((heads, BLK, 2 * BLK), F32),
            pltpu.VMEM((heads, 8, 2 * BLK), F32),
            pltpu.VMEM((heads, tokens, 2 * BLK), F32),
            pltpu.VMEM((tokens, width), F32),
            pltpu.VMEM((nx, tokens, width), BF16),
            pltpu.VMEM((BLK + 8, 2 * BLK), F32),
            pltpu.VMEM((BLK + 8, 2 * BLK), F32),
            pltpu.VMEM((ny, BLK + PRE, 2 * BLK), BF16),
            pltpu.VMEM((nz, BLK + PRE, 2 * BLK), BF16),
            pltpu.VMEM((BLK, BLK), F32),
            pltpu.VMEM((heads, BLK, BLK), F32),
            dma((7,)),
            dma((nx,)),
            dma((nx,)),
            dma((2, chunks)),
            dma((2, chunks)),
            dma((2, chunks)),
            dma((2, chunks)),
            dma((nx - 1,)),
            dma((nx - 1,)),
            dma((2,)),
            dma((2,)),
            dma((3,)),
            dma((3,)),
            dma((zc,)),
            dma((zc,)),
            dma((2, chunks)),
            dma((2, chunks)),
            dma((2, chunks)),
            dma((2, chunks)),
        ],
        compiler_params=pltpu.CompilerParams(
            collective_id=0, has_side_effects=True, vmem_limit_bytes=48 * 2**20
        ),
        name="layer",
    )(
        layer_in,
        query_weight,
        key_weight,
        value_weight,
        gate_weight,
        small,
        conv_weight,
        decay_log,
        beta_bias,
        decay_bias,
        norm_gain,
        out_weight,
    )


def solution(mesh):
    sizes = {"z": 8, "y": 4, "c": 2, "x": mesh.shape["head"]}
    finer = Mesh(
        mesh.devices.reshape(sizes["z"], sizes["y"], sizes["c"], sizes["x"]),
        ("z", "y", "c", "x"),
    )
    return jax.shard_map(
        functools.partial(on_device, sizes),
        mesh=finer,
        in_specs=(
            P(SEQ, "x"),
            P(None, "x"),
            P(None, "x"),
            P(None, "x"),
            P(None, "x"),
            P(None, "x"),
            P(None, "x"),
            P(None, None, "x"),
            P("x"),
            P("x"),
            P("x"),
            P(),
            P("x", None),
        ),
        out_specs=P(SEQ, "x"),
        check_vma=False,
    )
```

time: 233 us -> 85.1 us (0.37)
  the two profiles are of different devices: /device:TPU:8 before, /device:TPU:1 now
where the time goes in v1:
time: 85.1 us; the launch traced here: 84.9 us
  Pallas kernels  77.3 us (91%)
  local copies, waits for them, and re-layouts  6.1 us (7%)
  other arithmetic  1.38 us (2%)
    pallas_call x1, Pallas kernels, on_device(): pl.pallas_call(functools.partial(kernel, sizes), out_shape=jax.ShapeDtype...  77.3 us
    unnamed x26, local copies, waits for them, and re-layouts  6.02 us

profile of v1, /device:TPU:1, one launch (start us, length us, event | category | flops | bytes accessed | tf_op | source)
XLA Modules:
  0.0 84.9 jit_solution(17552234458661604956)
XLA Ops:
  0.0 0.0 copy-start.10
  0.0 0.0 copy-start.4
  0.0 1.1 %copy.14 = bf16[2048,2]{1,0:T(8,128)(2,1)S(1)} copy(bf16[2048,2]{0,1:T(2,128)(2,1)} %param.18) | data formatting | bytes 16384 | tf_op args[5]
  1.1 0.0 copy-done.10
  1.1 0.0 copy-start
  1.1 0.0 copy-start.1
  1.1 1.1 %copy.15 = bf16[2048,2]{1,0:T(8,128)(2,1)} copy(bf16[2048,2]{0,1:T(2,128)(2,1)S(1)} %copy-done.10) | data formatting | bytes 16384 | tf_op args[6]
  2.2 0.1 pad.2.clone
  2.2 0.0 copy-start.9
  2.2 1.4 %maximum_maximum_fusion.wbd = bf16[2048,128]{1,0:T(8,128)(2,1)S(1)} fusion(bf16[2048,2]{1,0:T(8,128)(2,1)} %copy.15, bf16[2048,2]{1,0:T(8,128)(2,1)S(1)} %copy.14, bf16[128]{0:T(256)(128)(2,1)S(1)} %pad.2.clone), kind=kLoop, calls=%fused_computation | loop fusion | flops 1572864 | bytes 540928 | tf_op jit(solution)/shard_map/concatenate | solution.py:562
  3.6 0.0 copy-done.9
  3.6 0.0 copy-start.5
  3.7 0.0 copy-start.6
  3.7 0.0 copy-start.7
  3.7 0.0 copy-start.8
  3.7 0.0 copy-done.4
  3.7 0.0 copy-done
  3.7 0.0 copy-done.1
  3.7 0.6 copy-done.5
  4.3 0.0 copy-done.6
  4.3 0.0 copy-done.7
  4.3 0.0 copy-done.8
  4.3 0.0 copy-start.2
  4.3 1.2 %copy-done.2 = bf16[2048,256]{1,0:T(8,128)(2,1)S(1)} copy-done((bf16[2048,256]{1,0:T(8,128)(2,1)S(1)}, bf16[2048,256]{1,0:T(8,128)(2,1)}, u32[]{:S(2)}) %copy-start.2) | copy-done | bytes 1048600
  5.6 0.0 copy-start.3
  5.6 1.2 %copy-done.3 = bf16[2048,256]{1,0:T(8,128)(2,1)S(1)} copy-done((bf16[2048,256]{1,0:T(8,128)(2,1)S(1)}, bf16[2048,256]{1,0:T(8,128)(2,1)}, u32[]{:S(2)}) %copy-start.3) | copy-done | bytes 1048600
  6.8 77.3 %layer.1 = bf16[512,512]{1,0:T(8,128)(2,1)S(1)} custom-call(bf16[512,512]{1,0:T(8,128)(2,1)S(1)} %copy-done.4, bf16[2048,256]{1,0:T(8,128)(2,1)S(1)} %copy-done, bf16[2048,256]{1,0:T(8,128)(2,1)S(1)} %copy-done.1, bf16[2048,256]{1,0:T(8,128)(2,1)S(1)} %copy-done.2, bf16[2048,256]{1,0:T(8,128)(2,1)S(1)} %copy-done.3, ...), custom_call_target="tpu_custom_call" | custom-call | tf_op jit(solution)/shard_map/layer/pallas_call | solution.py:575
  84.1 0.8 copy.18
  (2 shorter events, 0.0 us)
Async XLA Ops:
  0.0 1.1 %copy-start.10 = (bf16[2048,2]{0,1:T(2,128)(2,1)S(1)}, bf16[2048,2]{0,1:T(2,128)(2,1)}, u32[]{:S(2)}) copy-start(bf16[2048,2]{0,1:T(2,128)(2,1)} %param.19) | copy-start | bytes 24580
  0.0 3.7 %copy-start.4 = (bf16[512,512]{1,0:T(8,128)(2,1)S(1)}, bf16[512,512]{1,0:T(8,128)(2,1)}, u32[]{:S(2)}) copy-start(bf16[512,512]{1,0:T(8,128)(2,1)} %x_in.1) | copy-start | bytes 1572868
  1.1 2.6 %copy-start = (bf16[2048,256]{1,0:T(8,128)(2,1)S(1)}, bf16[2048,256]{1,0:T(8,128)(2,1)}, u32[]{:S(2)}) copy-start(bf16[2048,256]{1,0:T(8,128)(2,1)} %wq.1) | copy-start | bytes 3145732
  1.1 2.6 %copy-start.1 = (bf16[2048,256]{1,0:T(8,128)(2,1)S(1)}, bf16[2048,256]{1,0:T(8,128)(2,1)}, u32[]{:S(2)}) copy-start(bf16[2048,256]{1,0:T(8,128)(2,1)} %wk.1) | copy-start | bytes 3145732
  2.2 1.4 %copy-start.9 = (f32[4,3,256]{2,0,1:T(4,128)S(1)}, f32[4,3,256]{2,0,1:T(4,128)}, u32[]{:S(2)}) copy-start(f32[4,3,256]{2,0,1:T(4,128)} %param.20) | copy-start | bytes 36868
  3.6 0.7 copy-start.5
  3.7 0.7 copy-start.6
  3.7 0.7 copy-start.7
  3.7 0.7 copy-start.8
  4.3 1.2 %copy-start.2 = (bf16[2048,256]{1,0:T(8,128)(2,1)S(1)}, bf16[2048,256]{1,0:T(8,128)(2,1)}, u32[]{:S(2)}) copy-start(bf16[2048,256]{1,0:T(8,128)(2,1)} %wv.1) | copy-start | bytes 3145732
  5.6 1.2 %copy-start.3 = (bf16[2048,256]{1,0:T(8,128)(2,1)S(1)}, bf16[2048,256]{1,0:T(8,128)(2,1)}, u32[]{:S(2)}) copy-start(bf16[2048,256]{1,0:T(8,128)(2,1)} %wg.1) | copy-start | bytes 3145732

commit v2 on v1

--- a/solution.py
+++ b/solution.py
@@ -15,6 +15,7 @@
 BLK = 128
 HALF = BLK // 2
 PRE = 16
+PIECES = ((0, 80), (80, 64))
 NORM_FLOOR = 0.0001
 
 NN = (((1,), (0,)), ((), ()))
@@ -91,12 +92,13 @@
     wk,
     wv,
     wg,
-    wbd,
-    conv_w,
-    decay_log,
-    beta_bias,
-    decay_bias,
-    norm_gain,
+    wb_in,
+    wd_in,
+    conv_in,
+    decay_log_in,
+    beta_bias_in,
+    decay_bias_in,
+    norm_gain_in,
     w_out,
     out,
     xg,
@@ -113,6 +115,13 @@
     zb,
     fin_send,
     sin,
+    wb,
+    wd,
+    conv_w,
+    norm_gain,
+    decay_log,
+    beta_bias,
+    decay_bias,
     load_sem,
     pre_send,
     pre_recv,
@@ -162,13 +171,23 @@
         )
         cp.start()
         loads.append(cp)
-    cp = pltpu.make_async_copy(wbd, w_all.at[:, pl.ds(4 * width, BLK)], load_sem.at[5])
-    cp.start()
-    loads.append(cp)
+    small_loads = (
+        (wb_in, wb),
+        (wd_in, wd),
+        (conv_in, conv_w),
+        (norm_gain_in, norm_gain),
+        (decay_log_in, decay_log),
+        (beta_bias_in, beta_bias),
+        (decay_bias_in, decay_bias),
+    )
+    for i, (src, dst) in enumerate(small_loads):
+        cp = pltpu.make_async_copy(src, dst, load_sem.at[6 + i])
+        cp.start()
+        loads.append(cp)
     own_cols = pltpu.make_async_copy(
         w_out.at[:, pl.ds(pl.multiple_of(x * feats, feats), feats)],
         col_w.at[pl.ds(pl.multiple_of(x * width, width), width), :],
-        load_sem.at[6],
+        load_sem.at[5],
     )
     own_cols.start()
 
@@ -246,6 +265,17 @@
             direct(way, t).start()
     for cp in loads[1:]:
         cp.wait()
+    depth = wb.shape[1]
+    wide_row = lax.broadcasted_iota(jnp.int32, (8, BLK), 0)
+    for i in range(depth // BLK):
+        cols = slice(i * BLK, (i + 1) * BLK)
+        b_rows, d_rows = wb[:, cols].astype(F32), wd[:, cols].astype(F32)
+        tile = jnp.where(wide_row == 0, b_rows[0:1], 0.0)
+        tile = jnp.where(wide_row == 1, b_rows[1:2], tile)
+        tile = jnp.where(wide_row == 2, d_rows[0:1], tile)
+        tile = jnp.where(wide_row == 3, d_rows[1:2], tile)
+        tile = jnp.concatenate([tile, jnp.zeros((BLK - 8, BLK), F32)], axis=0)
+        w_all[cols, 4 * width :] = jnp.transpose(tile).astype(BF16)
 
     row_i = lax.broadcasted_iota(jnp.int32, (BLK, BLK), 0)
     col_i = lax.broadcasted_iota(jnp.int32, (BLK, BLK), 1)
@@ -275,7 +305,7 @@
         qkv = raw[:, 0 : 3 * width]
         qkv = jnp.where(jnp.logical_and(first, ext_row < PRE), 0.0, qkv)
         taps = [
-            jnp.concatenate([conv_w[s, i : i + 1, :] for i in range(3)], axis=1)
+            jnp.concatenate([conv_w[i, s : s + 1, :] for i in range(3)], axis=1)
             for s in range(4)
         ]
         mixed = taps[0] * qkv
@@ -325,19 +355,26 @@
                 jnp.concatenate([jnp.zeros_like(v), beta * v], axis=1) - read[:BLK]
             )
             both.append((low, mix, right_side, read[BLK:], kt, run_r, end, ext))
-        inv = [
-            jnp.where(row_i == col_i, 1.0, 0.0) - jnp.where(differ == 1, b[0], 0.0)
-            for b in both
-        ]
+        first_links = [jnp.where(differ == 1, b[0], 0.0) for b in both]
+        inv = [jnp.where(row_i == col_i, 1.0, 0.0) - m for m in first_links]
+        rest = []
+        for b, m in zip(both, first_links):
+            later = jnp.where(differ > 1, b[0], 0.0)
+            rest.append(later - dot3(later, m))
         w = 2
         while w < BLK:
             linking = jnp.logical_and(differ >= w, differ < 2 * w)
-            inv3 = [right3(a) for a in inv]
-            mids = [
-                dot1(left3(jnp.where(linking, b[0], 0.0)), a)
-                for b, a in zip(both, inv3)
-            ]
-            inv = [a - dot3(a, m) for a, m in zip(inv, mids)]
+            links = [right3(jnp.where(linking, r, 0.0)) for r in rest]
+            if 2 * w < BLK:
+                later = [jnp.where(differ >= 2 * w, r, 0.0) for r in rest]
+                stacked = [
+                    jnp.concatenate([r, a], axis=0) for r, a in zip(later, inv)
+                ]
+                moved = [s - dot1(left3(s), m) for s, m in zip(stacked, links)]
+                rest = [m[:BLK] for m in moved]
+                inv = [m[BLK:] for m in moved]
+            else:
+                inv = [a - dot1(left3(a), m) for a, m in zip(inv, links)]
             w *= 2
         for h in range(heads):
             low, mix, right_side, carried, kt, run_r, end, ext = both[h]
@@ -400,99 +437,136 @@
         keep = jnp.exp(logsum[h, 0:1, :])
         return (keep[:, :BLK] * eye - ext[:, :BLK], ext[:, BLK:], keep)
 
-    sl, sb, skeep = own_map(1 - c)
-    sc_send[0:BLK, 0:BLK] = sl
-    sc_send[0:BLK, BLK:] = sb
-    sc_send[BLK:, :] = jnp.broadcast_to(skeep, (8, 2 * BLK))
     swap = remote(sc_send, sc_recv, c_send.at[0], c_recv.at[0], {"c": 1 - c})
-    swap.start()
-    mine = own_map(c)
-    swap.wait()
-    other = (sc_recv[0:BLK, 0:BLK], sc_recv[0:BLK, BLK:], sc_recv[BLK : BLK + 1, :])
-    is_first = c == 0
-    map0 = pick(is_first, mine, other)
-    map1 = pick(is_first, other, mine)
-    chip_map = compose(map1, map0)
-
-    def put(buf, slot, m):
-        l, b, keep = m
-        buf[slot, 0:BLK, 0:BLK] = l.astype(BF16)
-        buf[slot, 0:BLK, BLK:] = b.astype(BF16)
-        hi, lo = halves(keep)
-        tail = lax.broadcasted_iota(jnp.int32, (PRE, 2 * BLK), 0)
-        buf[slot, BLK:, :] = jnp.where(
-            tail == 0, jnp.broadcast_to(hi.astype(F32), (PRE, 2 * BLK)),
-            jnp.broadcast_to(lo.astype(F32), (PRE, 2 * BLK)),
-        ).astype(BF16)
-
-    def get(buf, slot):
-        tail = buf[slot, BLK:, :].astype(F32)
-        return (
-            buf[slot, 0:BLK, 0:BLK].astype(F32),
-            buf[slot, 0:BLK, BLK:].astype(F32),
-            tail[0:1] + tail[1:2],
-        )
-
-    put(yb, y, chip_map)
-
-    def y_copy(slot, j, who):
-        return remote(yb.at[slot], yb.at[slot], y_send.at[j], y_recv.at[j], {"y": who})
-
-    y1 = y_copy(y, 0, up_y)
-    y2 = y_copy(y, 1, down_y)
-    y1.start()
-    y2.start()
-    y1.wait_recv()
-    y3 = y_copy(down_y, 2, up_y)
-    y3.start()
-    y2.wait_recv()
-    y3.wait_recv()
+    give = remote(fin_send, sin, c_send.at[1], c_recv.at[1], {"c": 1 - c})
+
+    @pl.when(c == 0)
+    def _():
+        for h in range(heads):
+            l, b, keep = own_map(h)
+            sc_send[h, 0:BLK, 0:BLK] = l
+            sc_send[h, 0:BLK, BLK:] = b
+            sc_send[h, BLK:, :] = jnp.broadcast_to(keep, (8, 2 * BLK))
+        swap.start()
+        swap.wait_send()
+        give.wait_recv()
+
     zero = jnp.zeros((BLK, BLK), F32)
     one_row = jnp.ones((1, 2 * BLK), F32)
     identity = (zero, zero, one_row)
-    maps = [get(yb, j) for j in range(ny)]
-    run = maps[0]
-    before_row = pick(y == 0, identity, run)
-    for j in range(1, ny):
-        before_row = pick(y == j, run, before_row) if j > 1 else before_row
-        run = compose(maps[j], run)
-
-    put(zb, z, run)
-
-    def z_copy(slot, j, who):
-        return remote(zb.at[slot], zb.at[slot], z_send.at[j], z_recv.at[j], {"z": who})
-
-    ups, downs = nz // 2, nz - 1 - nz // 2
-    near = identity
-    low_state = zero
-    flights = []
-    for j in range(ups):
-        cp = z_copy(lax.rem(z + nz - j, nz), j, up_z)
-        cp.start()
-        flights.append(cp)
-        dn = None
-        if j < downs:
-            dn = z_copy(lax.rem(z + j, nz), ups + j, down_z)
-            dn.start()
-            flights.append(dn)
-        if j > 0:
-            got = pick(z - j >= 0, get(zb, lax.rem(z + nz - j, nz)), identity)
-            near = compose(near, got)
-            if j <= downs:
-                got = pick(z + j - nz >= 0, get(zb, lax.rem(z + j, nz)), identity)
-                low_state = apply_map(got, low_state)
-        cp.wait_recv()
-        if dn is not None:
-            dn.wait_recv()
-    got = pick(z - ups >= 0, get(zb, lax.rem(z + nz - ups, nz)), identity)
-    row_state = apply_map(near, apply_map(got, low_state))
-    chip_state = apply_map(before_row, row_state)
-    later_state = apply_map(map0, chip_state)
-    sin[c] = jnp.where(is_first, chip_state, later_state)
-    fin_send[...] = jnp.where(is_first, later_state, chip_state)
-    give = remote(fin_send, sin.at[c], c_send.at[1], c_recv.at[1], {"c": 1 - c})
-    give.start()
-    give.wait()
+    each = range(heads)
+
+    def put(buf, slot, m, h):
+        l, b, keep = m
+        buf[slot, h, 0:BLK, 0:BLK] = l.astype(BF16)
+        buf[slot, h, 0:BLK, BLK:] = b.astype(BF16)
+        hi, lo = halves(keep)
+        tail = lax.broadcasted_iota(jnp.int32, (PRE, 2 * BLK), 0)
+        buf[slot, h, BLK:, :] = jnp.where(
+            tail == 0,
+            jnp.broadcast_to(hi.astype(F32), (PRE, 2 * BLK)),
+            jnp.broadcast_to(lo.astype(F32), (PRE, 2 * BLK)),
+        ).astype(BF16)
+
+    def get(buf, slot, h):
+        tail = buf[slot, h, BLK:, :].astype(F32)
+        return (
+            buf[slot, h, 0:BLK, 0:BLK].astype(F32),
+            buf[slot, h, 0:BLK, BLK:].astype(F32),
+            tail[0:1] + tail[1:2],
+        )
+
+    def pieces(buf, slot, send, recv, j, who):
+        made = []
+        for h in each:
+            for p, (at, rows) in enumerate(PIECES):
+                made.append(
+                    remote(
+                        buf.at[slot, h, pl.ds(at, rows), :],
+                        buf.at[slot, h, pl.ds(at, rows), :],
+                        send.at[j, h, p],
+                        recv.at[j, h, p],
+                        who,
+                    )
+                )
+        return made
+
+    @pl.when(c == 1)
+    def _():
+        own = [own_map(h) for h in each]
+        swap.wait_recv()
+        map0 = [
+            (sc_recv[h, 0:BLK, 0:BLK], sc_recv[h, 0:BLK, BLK:], sc_recv[h, BLK : BLK + 1, :])
+            for h in each
+        ]
+        for h in each:
+            put(yb, y, compose(own[h], map0[h]), h)
+
+        y1 = pieces(yb, y, y_send, y_recv, 0, {"y": up_y})
+        y2 = pieces(yb, y, y_send, y_recv, 1, {"y": down_y})
+        y3 = pieces(yb, down_y, y_send, y_recv, 2, {"y": up_y})
+        for a, b in zip(y1, y2):
+            a.start()
+            b.start()
+        for a, b in zip(y1, y3):
+            a.wait_recv()
+            b.start()
+        for b in y2:
+            b.wait_recv()
+        for b in y3:
+            b.wait_recv()
+        before_row = []
+        for h in each:
+            maps = [get(yb, j, h) for j in range(ny)]
+            run = maps[0]
+            prefix = pick(y == 0, identity, run)
+            for j in range(1, ny):
+                if j > 1:
+                    prefix = pick(y == j, run, prefix)
+                run = compose(maps[j], run)
+            before_row.append(prefix)
+            put(zb, z, run, h)
+
+        ups, downs = nz // 2, nz - 1 - nz // 2
+        up = [
+            pieces(zb, lax.rem(z + nz - j, nz), z_send, z_recv, j, {"z": up_z})
+            for j in range(ups)
+        ]
+        dn = [
+            pieces(zb, lax.rem(z + j, nz), z_send, z_recv, ups + j, {"z": down_z})
+            for j in range(downs)
+        ]
+        near = [identity] * heads
+        low_state = [zero] * heads
+        for a, b in zip(up[0], dn[0]):
+            a.start()
+            b.start()
+        for j in range(ups):
+            for p in range(len(up[0])):
+                up[j][p].wait_recv()
+                if j + 1 < ups:
+                    up[j + 1][p].start()
+                if j < downs:
+                    dn[j][p].wait_recv()
+                    if j + 1 < downs:
+                        dn[j + 1][p].start()
+            d = j + 1
+            for h in each:
+                got = pick(z - d >= 0, get(zb, lax.rem(z + nz - d, nz), h), identity)
+                if d < ups:
+                    near[h] = compose(near[h], got)
+                    got = pick(z + d - nz >= 0, get(zb, lax.rem(z + d, nz), h), identity)
+                    low_state[h] = apply_map(got, low_state[h])
+                else:
+                    row_state = apply_map(near[h], apply_map(got, low_state[h]))
+                    chip_state = apply_map(before_row[h], row_state)
+                    sin[h] = apply_map(map0[h], chip_state)
+                    fin_send[h] = chip_state
+        give.start()
+        give.wait_send()
+        for group in [y1, y2, y3] + up + dn:
+            for a in group:
+                a.wait_send()
 
     h_direct, h_relay = ring(hg, 0, hd_send, hd_recv, hf_send, hf_recv)
     starts = [right3(sin[h]) for h in range(heads)]
@@ -532,10 +606,6 @@
             h_relay(way, t).wait_send()
     for j in range(1, nx):
         columns(j).wait_send()
-    for cp in (y1, y2, y3):
-        cp.wait_send()
-    for cp in flights:
-        cp.wait_send()
 
 
 def on_device(
@@ -559,23 +629,14 @@
     nz, ny, nx = sizes["z"], sizes["y"], sizes["x"]
     chunks = tokens // BLK
     heads = 2
-    small = jnp.concatenate(
-        [
-            beta_weight,
-            decay_weight,
-            jnp.zeros((depth, BLK - 2 * heads), BF16),
-        ],
-        axis=1,
-    )
-    anyspace = pl.BlockSpec(memory_space=pl.ANY)
+    hbm = pl.BlockSpec(memory_space=pltpu.HBM)
     vmem = pl.BlockSpec(memory_space=pltpu.VMEM)
-    smem = pl.BlockSpec(memory_space=pltpu.SMEM)
     dma = pltpu.SemaphoreType.DMA
     zc = nz - 1
     return pl.pallas_call(
         functools.partial(kernel, sizes),
         out_shape=jax.ShapeDtypeStruct((tokens, feats), BF16),
-        in_specs=[anyspace] * 6 + [vmem] + [smem] * 3 + [vmem, anyspace],
+        in_specs=[hbm] * 13,
         out_specs=vmem,
         scratch_shapes=[
             pltpu.VMEM((nx, tokens + PRE, feats), BF16),
@@ -586,13 +647,20 @@
             pltpu.VMEM((heads, tokens, 2 * BLK), F32),
             pltpu.VMEM((tokens, width), F32),
             pltpu.VMEM((nx, tokens, width), BF16),
-            pltpu.VMEM((BLK + 8, 2 * BLK), F32),
-            pltpu.VMEM((BLK + 8, 2 * BLK), F32),
-            pltpu.VMEM((ny, BLK + PRE, 2 * BLK), BF16),
-            pltpu.VMEM((nz, BLK + PRE, 2 * BLK), BF16),
-            pltpu.VMEM((BLK, BLK), F32),
+            pltpu.VMEM((heads, BLK + 8, 2 * BLK), F32),
+            pltpu.VMEM((heads, BLK + 8, 2 * BLK), F32),
+            pltpu.VMEM((ny, heads, BLK + PRE, 2 * BLK), BF16),
+            pltpu.VMEM((nz, heads, BLK + PRE, 2 * BLK), BF16),
             pltpu.VMEM((heads, BLK, BLK), F32),
-            dma((7,)),
+            pltpu.VMEM((heads, BLK, BLK), F32),
+            pltpu.VMEM((heads, depth), BF16),
+            pltpu.VMEM((heads, depth), BF16),
+            pltpu.VMEM((3, 4, width), F32),
+            pltpu.VMEM((BLK,), F32),
+            pltpu.SMEM((heads,), F32),
+            pltpu.SMEM((heads,), F32),
+            pltpu.SMEM((heads,), F32),
+            dma((13,)),
             dma((nx,)),
             dma((nx,)),
             dma((2, chunks)),
@@ -603,17 +671,17 @@
             dma((nx - 1,)),
             dma((2,)),
             dma((2,)),
-            dma((3,)),
-            dma((3,)),
-            dma((zc,)),
-            dma((zc,)),
+            dma((3, heads, len(PIECES))),
+            dma((3, heads, len(PIECES))),
+            dma((zc, heads, len(PIECES))),
+            dma((zc, heads, len(PIECES))),
             dma((2, chunks)),
             dma((2, chunks)),
             dma((2, chunks)),
             dma((2, chunks)),
         ],
         compiler_params=pltpu.CompilerParams(
-            collective_id=0, has_side_effects=True, vmem_limit_bytes=48 * 2**20
+            collective_id=0, has_side_effects=True, vmem_limit_bytes=66519040
         ),
         name="layer",
     )(
@@ -622,8 +690,9 @@
         key_weight,
         value_weight,
         gate_weight,
-        small,
-        conv_weight,
+        beta_weight.T,
+        decay_weight.T,
+        conv_weight.transpose(1, 0, 2),
         decay_log,
         beta_bias,
         decay_bias,

time: 85.1 us -> 73.5 us (0.86)
  Pallas kernels: 77.3 us -> 71.5 us
  local copies, waits for them, and re-layouts: 6.1 us -> 1.87 us
  other arithmetic: 1.38 us -> 0 us
    pallas_call x1, Pallas kernels: 77.3 us -> 71.5 us  [on_device(): pl.pallas_call(functools.partial(kernel, sizes), out_shape=jax.ShapeDtype...]
    unnamed x26 -> x1, local copies, waits for them, and re-layouts: 6.02 us -> 1.87 us
    concatenate x1 -> x0, other arithmetic: 1.38 us -> none  [on_device(): jnp.concatenate([beta_weight, decay_weight, jnp.zeros((depth, BLK - 2 * h...]
where the time goes in v2:
time: 73.5 us; the launch traced here: 73.4 us
  Pallas kernels  71.5 us (97%)
  local copies, waits for them, and re-layouts  1.87 us (3%)
    pallas_call x1, Pallas kernels, on_device(): pl.pallas_call(functools.partial(kernel, sizes), out_shape=jax.ShapeDtype...  71.5 us
    unnamed x1, local copies, waits for them, and re-layouts  1.87 us

profile of v2, /device:TPU:1, one launch (start us, length us, event | category | flops | bytes accessed | tf_op | source)
XLA Modules:
  0.0 73.4 jit_solution(3438289209375020666)
XLA Ops:
  0.0 71.5 %layer.1 = bf16[512,512]{1,0:T(8,128)(2,1)} custom-call(bf16[512,512]{1,0:T(8,128)(2,1)} %x_in.1, bf16[2048,256]{1,0:T(8,128)(2,1)} %wq.1, bf16[2048,256]{1,0:T(8,128)(2,1)} %wk.1, bf16[2048,256]{1,0:T(8,128)(2,1)} %wv.1, bf16[2048,256]{1,0:T(8,128)(2,1)} %wg.1, bf16[2,2048]{1,0:T(2,128)(2,1)} %bitcast.4, bf16[2,2048]{1,0:T(2,128)(2,1)} %bitcast.5, ...), custom_call_target="tpu_custom_call" | custom-call | tf_op jit(solution)/shard_map/layer/pallas_call | solution.py:636
  71.5 1.9 %copy.15 = bf16[512,512]{1,0:T(8,128)(2,1)} copy(bf16[512,512]{1,0:T(8,128)(2,1)} %layer.1) | data formatting | bytes 1048576

commit v3 on v2

--- a/solution.py
+++ b/solution.py
@@ -15,6 +15,7 @@
 BLK = 128
 HALF = BLK // 2
 PRE = 16
+SENT = 8
 PIECES = ((0, 80), (80, 64))
 NORM_FLOOR = 0.0001
 
@@ -45,11 +46,18 @@
     return dot1(left3(a), right3(b))
 
 
-def dot_exact_left(a_bf16, b):
-    hi, lo = halves(b)
-    return dot1(
-        jnp.concatenate([a_bf16, a_bf16], axis=1), jnp.concatenate([hi, lo], axis=0)
-    )
+def product(a, b, exact_a=False, exact_b=False):
+    if exact_a and exact_b:
+        return dot1(a.astype(BF16), b.astype(BF16))
+    if exact_a:
+        hi, lo = halves(b)
+        a = a.astype(BF16)
+        return dot1(jnp.concatenate([a, a], axis=1), jnp.concatenate([hi, lo], axis=0))
+    if exact_b:
+        hi, lo = halves(a)
+        b = b.astype(BF16)
+        return dot1(jnp.concatenate([hi, lo], axis=1), jnp.concatenate([b, b], axis=0))
+    return dot3(a, b)
 
 
 def sigmoid(v):
@@ -64,10 +72,10 @@
     return jnp.maximum(v, 0.0) + jnp.log(1.0 + jnp.exp(-jnp.abs(v)))
 
 
-def compose(later, earlier):
+def compose(later, earlier, *exact):
     l2, b2, c2 = later
     l1, b1, c1 = earlier
-    moved = dot3(l2, jnp.concatenate([l1, b1], axis=1))
+    moved = product(l2, jnp.concatenate([l1, b1], axis=1), *exact)
     width = l1.shape[1]
     return (
         c2[:, :width] * l1 + c1[:, :width] * l2 - moved[:, :width],
@@ -76,9 +84,9 @@
     )
 
 
-def apply_map(m, state):
+def apply_map(m, state, *exact):
     l, b, c = m
-    return c[:, : state.shape[1]] * state - dot3(l, state) + b
+    return c[:, : state.shape[1]] * state - product(l, state, *exact) + b
 
 
 def pick(flag, m, other):
@@ -131,6 +139,8 @@
     f_recv,
     w_send,
     w_recv,
+    hand_send,
+    hand_recv,
     c_send,
     c_recv,
     y_send,
@@ -161,6 +171,8 @@
 
     def place(s, xx):
         return {"z": s // (ny * 2), "y": lax.rem(s // 2, ny), "c": lax.rem(s, 2), "x": xx}
+
+    xg[:, 0:PRE, :] = jnp.zeros((nx, PRE, feats), BF16)
 
     weights = (wq, wk, wv, wg)
     loads = [pltpu.make_async_copy(x_in, xg.at[x, pl.ds(PRE, tokens), :], load_sem.at[0])]
@@ -251,8 +263,8 @@
 
     def pre_copy(i):
         return remote(
-            xg.at[x, pl.ds(tokens, PRE), :],
-            xg.at[x, pl.ds(0, PRE), :],
+            xg.at[x, pl.ds(tokens + SENT, SENT), :],
+            xg.at[x, pl.ds(SENT, SENT), :],
             pre_send.at[i],
             pre_recv.at[x],
             place(after, i),
@@ -402,8 +414,8 @@
         def _():
             for i in range(nx):
                 remote(
-                    xg.at[i, pl.ds(tokens, PRE), :],
-                    xg.at[i, pl.ds(0, PRE), :],
+                    xg.at[i, pl.ds(tokens + SENT, SENT), :],
+                    xg.at[i, pl.ds(SENT, SENT), :],
                     pre_send.at[i],
                     pre_recv.at[i],
                     place(after, i),
@@ -429,8 +441,21 @@
             {"x": who},
         )
 
-    for j in range(1, nx):
-        columns(j).start()
+    def handed(j):
+        rows = pl.ds(pl.multiple_of(lax.rem(x + nx - j, nx) * width, width), width)
+        return remote(
+            col_w.at[rows, :],
+            col_w.at[rows, :],
+            hand_send.at[j - 1],
+            hand_recv.at[j - 1],
+            {"c": 1 - c},
+        )
+
+    @pl.when(c == 0)
+    def _():
+        for j in range(1, nx):
+            columns(j).start()
+
 
     def own_map(h):
         ext = state[h]
@@ -449,6 +474,12 @@
             sc_send[h, BLK:, :] = jnp.broadcast_to(keep, (8, 2 * BLK))
         swap.start()
         swap.wait_send()
+        for j in range(1, nx):
+            columns(j).wait_recv()
+            handed(j).start()
+        for j in range(1, nx):
+            columns(j).wait_send()
+            handed(j).wait_send()
         give.wait_recv()
 
     zero = jnp.zeros((BLK, BLK), F32)
@@ -518,12 +549,13 @@
         before_row = []
         for h in each:
             maps = [get(yb, j, h) for j in range(ny)]
-            run = maps[0]
-            prefix = pick(y == 0, identity, run)
-            for j in range(1, ny):
-                if j > 1:
-                    prefix = pick(y == j, run, prefix)
-                run = compose(maps[j], run)
+            low_pair = compose(maps[1], maps[0], True, True)
+            high_pair = compose(maps[3], maps[2], True, True)
+            triple = compose(maps[2], low_pair, True)
+            run = compose(high_pair, low_pair)
+            prefix = pick(y == 0, identity, maps[0])
+            prefix = pick(y == 2, low_pair, prefix)
+            prefix = pick(y == 3, triple, prefix)
             before_row.append(prefix)
             put(zb, z, run, h)
 
@@ -538,6 +570,7 @@
         ]
         near = [identity] * heads
         low_state = [zero] * heads
+        own_near = [identity] * heads
         for a, b in zip(up[0], dn[0]):
             a.start()
             b.start()
@@ -554,14 +587,16 @@
             for h in each:
                 got = pick(z - d >= 0, get(zb, lax.rem(z + nz - d, nz), h), identity)
                 if d < ups:
-                    near[h] = compose(near[h], got)
+                    near[h] = compose(near[h], got, False, True)
                     got = pick(z + d - nz >= 0, get(zb, lax.rem(z + d, nz), h), identity)
-                    low_state[h] = apply_map(got, low_state[h])
+                    low_state[h] = apply_map(got, low_state[h], True)
+                    if d == ups - 1:
+                        near[h] = compose(before_row[h], near[h])
+                        own_near[h] = compose(map0[h], near[h])
                 else:
-                    row_state = apply_map(near[h], apply_map(got, low_state[h]))
-                    chip_state = apply_map(before_row[h], row_state)
-                    sin[h] = apply_map(map0[h], chip_state)
-                    fin_send[h] = chip_state
+                    row_state = apply_map(got, low_state[h], True)
+                    fin_send[h] = apply_map(near[h], row_state)
+                    sin[h] = apply_map(own_near[h], row_state)
         give.start()
         give.wait_send()
         for group in [y1, y2, y3] + up + dn:
@@ -587,8 +622,11 @@
             h_direct(way, t).wait_recv()
             h_relay(way, t).start()
     own_cols.wait()
-    for j in range(1, nx):
-        columns(j).wait_recv()
+    @pl.when(c == 1)
+    def _():
+        for j in range(1, nx):
+            handed(j).wait_recv()
+
     for t in range(chunks):
         rows = slice(t * BLK, (t + 1) * BLK)
         for way in range(2):
@@ -604,8 +642,6 @@
             relay(way, t).wait_send()
             h_direct(way, t).wait_send()
             h_relay(way, t).wait_send()
-    for j in range(1, nx):
-        columns(j).wait_send()
 
 
 def on_device(
@@ -635,7 +671,7 @@
     zc = nz - 1
     return pl.pallas_call(
         functools.partial(kernel, sizes),
-        out_shape=jax.ShapeDtypeStruct((tokens, feats), BF16),
+        out_shape=pltpu.VMEM((tokens, feats), BF16),
         in_specs=[hbm] * 13,
         out_specs=vmem,
         scratch_shapes=[
@@ -669,6 +705,8 @@
             dma((2, chunks)),
             dma((nx - 1,)),
             dma((nx - 1,)),
+            dma((nx - 1,)),
+            dma((nx - 1,)),
             dma((2,)),
             dma((2,)),
             dma((3, heads, len(PIECES))),

time: 73.5 us -> 70.6 us (0.961)
  Pallas kernels: 71.5 us -> 69.7 us
  local copies, waits for them, and re-layouts: 1.87 us -> 0.8 us
    pallas_call x1, Pallas kernels: 71.5 us -> 69.7 us  [on_device(): pl.pallas_call(functools.partial(kernel, sizes), out_shape=pltpu.VMEM((to...]
    unnamed x1, local copies, waits for them, and re-layouts: 1.87 us -> 0.8 us
where the time goes in v3:
time: 70.6 us; the launch traced here: 70.5 us
  Pallas kernels  69.7 us (99%)
  local copies, waits for them, and re-layouts  0.8 us (1%)
    pallas_call x1, Pallas kernels, on_device(): pl.pallas_call(functools.partial(kernel, sizes), out_shape=pltpu.VMEM((to...  69.7 us

profile of v3, /device:TPU:1, one launch (start us, length us, event | category | flops | bytes accessed | tf_op | source)
XLA Modules:
  0.0 70.5 jit_solution(12438834653127660985)
XLA Ops:
  0.0 69.7 %layer.1 = bf16[512,512]{1,0:T(8,128)(2,1)S(1)} custom-call(bf16[512,512]{1,0:T(8,128)(2,1)} %x_in.1, bf16[2048,256]{1,0:T(8,128)(2,1)} %wq.1, bf16[2048,256]{1,0:T(8,128)(2,1)} %wk.1, bf16[2048,256]{1,0:T(8,128)(2,1)} %wv.1, bf16[2048,256]{1,0:T(8,128)(2,1)} %wg.1, bf16[2,2048]{1,0:T(2,128)(2,1)} %bitcast.4, bf16[2,2048]{1,0:T(2,128)(2,1)} %bitcast.5, ...), custom_call_target="tpu_custom_call" | custom-call | tf_op jit(solution)/shard_map/layer/pallas_call | solution.py:672
  69.7 0.8 %copy.15 = bf16[512,512]{1,0:T(8,128)(2,1)} copy(bf16[512,512]{1,0:T(8,128)(2,1)S(1)} %layer.1) | data formatting | bytes 1048576

commit v4 on v3

--- a/solution.py
+++ b/solution.py
@@ -151,6 +151,7 @@
     hd_recv,
     hf_send,
     hf_recv,
+    ready,
 ):
     nz, ny, nx = sizes["z"], sizes["y"], sizes["x"]
     z = lax.axis_index("z")
@@ -206,12 +207,41 @@
     barrier = pltpu.get_barrier_semaphore()
     up_y, down_y = lax.rem(y + 1, ny), lax.rem(y + ny - 1, ny)
     up_z, down_z = lax.rem(z + 1, nz), lax.rem(z + nz - 1, nz)
-    partners = [{"x": right}, {"x": left}, {"x": far}, {"c": 1 - c}]
-    partners += [{"y": up_y}, {"y": down_y}, {"z": up_z}, {"z": down_z}]
-    partners += [place(after, i) for i in range(nx)]
-    partners += [place(prior, i) for i in range(nx)]
-    for who in partners:
+    last_z = nz - 1
+    has_after = here < count - 1
+    has_prior = here > 0
+
+    def enter(who):
         pl.semaphore_signal(barrier, inc=1, device_id=who, device_id_type=MESH)
+
+    always = [{"x": right}, {"x": left}, {"x": far}, {"c": 1 - c}, {"y": up_y}, {"y": down_y}]
+    for who in always:
+        enter(who)
+
+    @pl.when(has_prior)
+    def _():
+        for i in range(nx):
+            enter(place(prior, i))
+
+    @pl.when(z > 0)
+    def _():
+        enter({"z": down_z})
+
+    @pl.when(z < last_z)
+    def _():
+        enter({"z": up_z})
+
+    @pl.when(z == 0)
+    def _():
+        enter({"z": down_z})
+
+    expected = (
+        len(always)
+        + nx * has_after.astype(jnp.int32)
+        + (z < last_z).astype(jnp.int32)
+        + (z > 0).astype(jnp.int32)
+        + (z == last_z).astype(jnp.int32)
+    )
 
     state[...] = jnp.zeros_like(state)
     eye = (
@@ -221,7 +251,12 @@
     for h in range(heads):
         state[h, :, 0:BLK] = eye
     logsum[...] = jnp.zeros_like(logsum)
-    pl.semaphore_wait(barrier, len(partners))
+    pl.semaphore_wait(barrier, expected)
+
+    @pl.when(jnp.logical_and(z == last_z, c == 1))
+    def _():
+        pl.semaphore_signal(ready, inc=1, device_id={"z": up_z}, device_id_type=MESH)
+
     loads[0].wait()
 
     def remote(src, dst, send, recv, who):
@@ -270,8 +305,11 @@
             place(after, i),
         )
 
-    for i in range(nx):
-        pre_copy(i).start()
+    @pl.when(has_after)
+    def _():
+        for i in range(nx):
+            pre_copy(i).start()
+
     for t in range(2):
         for way in range(2):
             direct(way, t).start()
@@ -410,7 +448,7 @@
             direct(0, t + 2).start()
             direct(1, t + 2).start()
 
-        @pl.when(t == 0)
+        @pl.when(jnp.logical_and(t == 0, has_prior))
         def _():
             for i in range(nx):
                 remote(
@@ -571,18 +609,41 @@
         near = [identity] * heads
         low_state = [zero] * heads
         own_near = [identity] * heads
-        for a, b in zip(up[0], dn[0]):
-            a.start()
-            b.start()
+        def guarded(flag, copies, wait=False):
+            @pl.when(flag)
+            def _():
+                for a in copies:
+                    if wait:
+                        a.wait_send()
+                    else:
+                        a.start()
+
+        sends_up = [jnp.logical_and(z < last_z, z >= j) for j in range(ups)]
+        sends_dn = [lax.rem(z + j, nz) < downs for j in range(downs)]
+        guarded(sends_up[0], up[0])
+
+        @pl.when(z == 0)
+        def _():
+            pl.semaphore_wait(ready, 1)
+
+        guarded(sends_dn[0], dn[0])
         for j in range(ups):
             for p in range(len(up[0])):
-                up[j][p].wait_recv()
+
+                @pl.when(z > j)
+                def _():
+                    up[j][p].wait_recv()
+
                 if j + 1 < ups:
-                    up[j + 1][p].start()
+                    guarded(sends_up[j + 1], [up[j + 1][p]])
                 if j < downs:
-                    dn[j][p].wait_recv()
-                    if j + 1 < downs:
-                        dn[j + 1][p].start()
+
+                    @pl.when(lax.rem(z + 1 + j, nz) < downs)
+                    def _():
+                        dn[j][p].wait_recv()
+                        if j + 1 < downs:
+                            dn[j + 1][p].start()
+
             d = j + 1
             for h in each:
                 got = pick(z - d >= 0, get(zb, lax.rem(z + nz - d, nz), h), identity)
@@ -599,9 +660,13 @@
                     sin[h] = apply_map(own_near[h], row_state)
         give.start()
         give.wait_send()
-        for group in [y1, y2, y3] + up + dn:
+        for group in [y1, y2, y3]:
             for a in group:
                 a.wait_send()
+        for j in range(ups):
+            guarded(sends_up[j], up[j], True)
+        for j in range(downs):
+            guarded(sends_dn[j], dn[j], True)
 
     h_direct, h_relay = ring(hg, 0, hd_send, hd_recv, hf_send, hf_recv)
     starts = [right3(sin[h]) for h in range(heads)]
@@ -634,8 +699,11 @@
         rows_all = jnp.concatenate([hg[p, rows, :] for p in range(nx)], axis=1)
         out[rows, :] = dot1(rows_all, col_w[...]).astype(BF16)
 
-    for i in range(nx):
-        pre_copy(i).wait_send()
+    @pl.when(has_after)
+    def _():
+        for i in range(nx):
+            pre_copy(i).wait_send()
+
     for t in range(chunks):
         for way in range(2):
             direct(way, t).wait_send()
@@ -717,6 +785,7 @@
             dma((2, chunks)),
             dma((2, chunks)),
             dma((2, chunks)),
+            pltpu.SemaphoreType.REGULAR,
         ],
         compiler_params=pltpu.CompilerParams(
             collective_id=0, has_side_effects=True, vmem_limit_bytes=66519040

time: 70.6 us -> 64.7 us (0.916); the launches traced: 70.5 us -> 63.8 us
  Pallas kernels: 69.7 us -> 63 us
    pallas_call x1, Pallas kernels: 69.7 us -> 63 us  [on_device(): pl.pallas_call(functools.partial(kernel, sizes), out_shape=pltpu.VMEM((to...]
where the time goes in v4:
time: 64.7 us; the launch traced here: 63.8 us
  Pallas kernels  63 us (97%)
  local copies, waits for them, and re-layouts  0.8 us (1%)
    pallas_call x1, Pallas kernels, on_device(): pl.pallas_call(functools.partial(kernel, sizes), out_shape=pltpu.VMEM((to...  63 us

profile of v4, /device:TPU:1, one launch (start us, length us, event | category | flops | bytes accessed | tf_op | source)
XLA Modules:
  0.0 63.8 jit_solution(10466279033994970918)
XLA Ops:
  0.0 63.0 %layer.1 = bf16[512,512]{1,0:T(8,128)(2,1)S(1)} custom-call(bf16[512,512]{1,0:T(8,128)(2,1)} %x_in.1, bf16[2048,256]{1,0:T(8,128)(2,1)} %wq.1, bf16[2048,256]{1,0:T(8,128)(2,1)} %wk.1, bf16[2048,256]{1,0:T(8,128)(2,1)} %wv.1, bf16[2048,256]{1,0:T(8,128)(2,1)} %wg.1, bf16[2,2048]{1,0:T(2,128)(2,1)} %bitcast.4, bf16[2,2048]{1,0:T(2,128)(2,1)} %bitcast.5, ...), custom_call_target="tpu_custom_call" | custom-call | tf_op jit(solution)/shard_map/layer/pallas_call | solution.py:740
  63.0 0.8 %copy.15 = bf16[512,512]{1,0:T(8,128)(2,1)} copy(bf16[512,512]{1,0:T(8,128)(2,1)S(1)} %layer.1) | data formatting | bytes 1048576

commit v5 on v4

--- a/solution.py
+++ b/solution.py
@@ -16,7 +16,7 @@
 HALF = BLK // 2
 PRE = 16
 SENT = 8
-PIECES = ((0, 80), (80, 64))
+PIECES = ((0, 48), (48, 48), (96, 48))
 NORM_FLOOR = 0.0001
 
 NN = (((1,), (0,)), ((), ()))
@@ -130,6 +130,12 @@
     decay_log,
     beta_bias,
     decay_bias,
+    kept_q,
+    kept_g,
+    kept_total,
+    kept_kt,
+    kept_state,
+    kept_u,
     load_sem,
     pre_send,
     pre_recv,
@@ -295,6 +301,18 @@
         return direct, relay
 
     direct, relay = ring(xg, PRE, d_send, d_recv, f_send, f_recv)
+    final = chunks - 1
+
+    def last(way, p):
+        half = way if p == 0 else 1 - way
+        rows = pl.ds(PRE + final * BLK + half * HALF, HALF)
+        return remote(
+            xg.at[x, rows, :],
+            xg.at[x, rows, :],
+            d_send.at[way, final + p],
+            d_recv.at[way, final + p],
+            {"x": (right, left)[way]},
+        )
 
     def pre_copy(i):
         return remote(
@@ -345,6 +363,16 @@
     def unit_rows(v):
         return v * lax.rsqrt(jnp.sum(v * v, axis=-1, keepdims=True) + 1.0)
 
+    def mix_taps(which, values):
+        taps = [
+            jnp.concatenate([conv_w[i, s : s + 1, :] for i in which], axis=1)
+            for s in range(4)
+        ]
+        mixed = taps[0] * values
+        for s in range(1, 4):
+            mixed = mixed + taps[s] * pltpu.roll(values, s, 0)
+        return silu(mixed[PRE:])
+
     def chunk(t):
         start = pl.multiple_of(t * BLK, BLK)
         rows = pl.ds(start, BLK + PRE)
@@ -354,20 +382,9 @@
         raw = dot1(xs, w_all[...])
         qkv = raw[:, 0 : 3 * width]
         qkv = jnp.where(jnp.logical_and(first, ext_row < PRE), 0.0, qkv)
-        taps = [
-            jnp.concatenate([conv_w[i, s : s + 1, :] for i in range(3)], axis=1)
-            for s in range(4)
-        ]
-        mixed = taps[0] * qkv
-        for s in range(1, 4):
-            mixed = mixed + taps[s] * pltpu.roll(qkv, s, 0)
-        mixed = silu(mixed[PRE:])
-        out_rows = pl.ds(start, BLK)
-        gates = silu(raw[PRE:, 3 * width : 4 * width])
-        for h in range(heads):
-            gate[out_rows, h * BLK : (h + 1) * BLK] = (
-                gates[:, h * BLK : (h + 1) * BLK] * gain_row
-            )
+        kept_q[t] = qkv[:, 0:width]
+        kept_g[t] = raw[PRE:, 3 * width : 4 * width]
+        mixed = mix_taps((1, 2), qkv[:, width:])
         small = raw[PRE:, 4 * width :] + bias_row
         betas = sigmoid(small)
         steps = -rate_row * softplus(small)
@@ -381,72 +398,109 @@
             jnp.concatenate([s_hi, s_mid, s_lo], axis=0),
         )
         total_t = jnp.transpose(total)
+        kept_total[t, 0] = total
+        kept_total[t, 1] = total_t
         both = []
         for h in range(heads):
-            cols = slice(h * BLK, (h + 1) * BLK)
-            q = unit_rows(mixed[:, h * BLK : (h + 1) * BLK])
-            k = unit_rows(mixed[:, width + h * BLK : width + (h + 1) * BLK])
-            v = mixed[:, 2 * width + h * BLK : 2 * width + (h + 1) * BLK]
+            k = unit_rows(mixed[:, h * BLK : (h + 1) * BLK])
+            v = mixed[:, width + h * BLK : width + (h + 1) * BLK]
             beta = betas[:, h : h + 1]
             run_c = total[:, 2 + h : 3 + h]
             run_r = total_t[2 + h : 3 + h, :]
             end = run_r[:, BLK - 1 : BLK]
             decay = jnp.where(within, jnp.exp(jnp.minimum(run_c - run_r, 0.0)), 0.0)
             kt = jnp.transpose(k)
-            scores = dot3(jnp.concatenate([k, q], axis=0), kt)
-            low = jnp.where(before, beta * decay * scores[:BLK], 0.0)
-            mix = decay * scores[BLK:]
-            grow = jnp.exp(run_c)
+            low = jnp.where(before, beta * decay * dot3(k, kt), 0.0)
             ext = state[h]
-            read = dot3(
-                jnp.concatenate([(beta * grow) * k, grow * q], axis=0), ext
-            )
-            right_side = (
-                jnp.concatenate([jnp.zeros_like(v), beta * v], axis=1) - read[:BLK]
-            )
-            both.append((low, mix, right_side, read[BLK:], kt, run_r, end, ext))
+            read = dot3((beta * jnp.exp(run_c)) * k, ext)
+            right_side = jnp.concatenate([jnp.zeros_like(v), beta * v], axis=1) - read
+            kept_kt[t, h] = kt
+            kept_state[t, h] = ext
+            both.append((low, right_side, kt, run_r, end, ext))
         first_links = [jnp.where(differ == 1, b[0], 0.0) for b in both]
         inv = [jnp.where(row_i == col_i, 1.0, 0.0) - m for m in first_links]
         rest = []
         for b, m in zip(both, first_links):
             later = jnp.where(differ > 1, b[0], 0.0)
-            rest.append(later - dot3(later, m))
+            rest.append(later - product(later, m, False, True))
         w = 2
         while w < BLK:
             linking = jnp.logical_and(differ >= w, differ < 2 * w)
-            links = [right3(jnp.where(linking, r, 0.0)) for r in rest]
+            links = [jnp.where(linking, r, 0.0) for r in rest]
             if 2 * w < BLK:
                 later = [jnp.where(differ >= 2 * w, r, 0.0) for r in rest]
                 stacked = [
                     jnp.concatenate([r, a], axis=0) for r, a in zip(later, inv)
                 ]
-                moved = [s - dot1(left3(s), m) for s, m in zip(stacked, links)]
+                moved = [
+                    s - product(s, m, False, True) for s, m in zip(stacked, links)
+                ]
                 rest = [m[:BLK] for m in moved]
                 inv = [m[BLK:] for m in moved]
             else:
-                inv = [a - dot1(left3(a), m) for a, m in zip(inv, links)]
+                inv = [a - product(a, m, False, True) for a, m in zip(inv, links)]
             w *= 2
         for h in range(heads):
-            low, mix, right_side, carried, kt, run_r, end, ext = both[h]
+            low, right_side, kt, run_r, end, ext = both[h]
             solved = dot3(inv[h], right_side)
-            solved3 = right3(solved)
-            prelim[h, out_rows, :] = carried + dot1(left3(mix), solved3)
+            kept_u[t, h] = solved
             weighted = kt * jnp.exp(end - run_r)
-            state[h] = jnp.exp(end) * ext + dot1(left3(weighted), solved3)
+            state[h] = jnp.exp(end) * ext + dot3(weighted, solved)
             logsum[h] = logsum[h] + jnp.broadcast_to(end, logsum.shape[1:])
 
+    def reading(t):
+        start = t * BLK if isinstance(t, int) else pl.multiple_of(t * BLK, BLK)
+        out_rows = pl.ds(start, BLK)
+        gates = silu(kept_g[t])
+        mixed = mix_taps((0,), kept_q[t])
+        total, total_t = kept_total[t, 0], kept_total[t, 1]
+        for h in range(heads):
+            cols = slice(h * BLK, (h + 1) * BLK)
+            gate[out_rows, cols] = gates[:, cols] * gain_row
+            q = unit_rows(mixed[:, cols])
+            run_c = total[:, 2 + h : 3 + h]
+            run_r = total_t[2 + h : 3 + h, :]
+            decay = jnp.where(within, jnp.exp(jnp.minimum(run_c - run_r, 0.0)), 0.0)
+            mix = decay * dot3(q, kept_kt[t, h])
+            prelim[h, out_rows, :] = dot3(jnp.exp(run_c) * q, kept_state[t, h]) + dot3(
+                mix, kept_u[t, h]
+            )
+
     def step(t, carry):
-        @pl.when(t < chunks)
+        @pl.when(t < final)
         def _():
             direct(0, t).wait_recv()
             direct(1, t).wait_recv()
+
+        @pl.when(t == final)
+        def _():
+            last(0, 0).wait_recv()
+            last(1, 0).wait_recv()
+
+        @pl.when(t < chunks)
+        def _():
             relay(0, t).start()
             relay(1, t).start()
 
-        @pl.when(t < chunks - 2)
+        @pl.when(t < final - 2)
         def _():
             direct(0, t + 2).start()
             direct(1, t + 2).start()
+
+        @pl.when(t == final - 2)
+        def _():
+            last(0, 0).start()
+            last(1, 0).start()
+
+        @pl.when(t == final - 1)
+        def _():
+            last(0, 1).start()
+            last(1, 1).start()
+
+        @pl.when(t == chunks)
+        def _():
+            last(0, 1).wait_recv()
+            last(1, 1).wait_recv()
 
         @pl.when(jnp.logical_and(t == 0, has_prior))
         def _():
@@ -458,6 +512,10 @@
                     pre_recv.at[i],
                     place(after, i),
                 ).wait_recv()
+
+        @pl.when(jnp.logical_and(t > 1, t < chunks))
+        def _():
+            reading(t - 2)
 
         @pl.when(t > 0)
         def _():
@@ -511,6 +569,8 @@
             sc_send[h, 0:BLK, BLK:] = b
             sc_send[h, BLK:, :] = jnp.broadcast_to(keep, (8, 2 * BLK))
         swap.start()
+        reading(chunks - 2)
+        reading(chunks - 1)
         swap.wait_send()
         for j in range(1, nx):
             columns(j).wait_recv()
@@ -568,34 +628,23 @@
             (sc_recv[h, 0:BLK, 0:BLK], sc_recv[h, 0:BLK, BLK:], sc_recv[h, BLK : BLK + 1, :])
             for h in each
         ]
-        for h in each:
-            put(yb, y, compose(own[h], map0[h]), h)
-
         y1 = pieces(yb, y, y_send, y_recv, 0, {"y": up_y})
         y2 = pieces(yb, y, y_send, y_recv, 1, {"y": down_y})
         y3 = pieces(yb, down_y, y_send, y_recv, 2, {"y": up_y})
-        for a, b in zip(y1, y2):
-            a.start()
-            b.start()
+        many = len(PIECES)
+
+        def of_head(copies, h):
+            return copies[h * many : (h + 1) * many]
+
+        for h in each:
+            put(yb, y, compose(own[h], map0[h]), h)
+            for a, b in zip(of_head(y1, h), of_head(y2, h)):
+                a.start()
+                b.start()
+        reading(chunks - 2)
         for a, b in zip(y1, y3):
             a.wait_recv()
             b.start()
-        for b in y2:
-            b.wait_recv()
-        for b in y3:
-            b.wait_recv()
-        before_row = []
-        for h in each:
-            maps = [get(yb, j, h) for j in range(ny)]
-            low_pair = compose(maps[1], maps[0], True, True)
-            high_pair = compose(maps[3], maps[2], True, True)
-            triple = compose(maps[2], low_pair, True)
-            run = compose(high_pair, low_pair)
-            prefix = pick(y == 0, identity, maps[0])
-            prefix = pick(y == 2, low_pair, prefix)
-            prefix = pick(y == 3, triple, prefix)
-            before_row.append(prefix)
-            put(zb, z, run, h)
 
         ups, downs = nz // 2, nz - 1 - nz // 2
         up = [
@@ -620,13 +669,27 @@
 
         sends_up = [jnp.logical_and(z < last_z, z >= j) for j in range(ups)]
         sends_dn = [lax.rem(z + j, nz) < downs for j in range(downs)]
-        guarded(sends_up[0], up[0])
 
         @pl.when(z == 0)
         def _():
             pl.semaphore_wait(ready, 1)
 
-        guarded(sends_dn[0], dn[0])
+        before_row = []
+        for h in each:
+            for b in of_head(y2, h) + of_head(y3, h):
+                b.wait_recv()
+            maps = [get(yb, j, h) for j in range(ny)]
+            low_pair = compose(maps[1], maps[0], True, True)
+            high_pair = compose(maps[3], maps[2], True, True)
+            triple = compose(maps[2], low_pair, True)
+            put(zb, z, compose(high_pair, low_pair), h)
+            guarded(sends_up[0], of_head(up[0], h))
+            guarded(sends_dn[0], of_head(dn[0], h))
+            prefix = pick(y == 0, identity, maps[0])
+            prefix = pick(y == 2, low_pair, prefix)
+            prefix = pick(y == 3, triple, prefix)
+            before_row.append(prefix)
+        reading(chunks - 1)
         for j in range(ups):
             for p in range(len(up[0])):
 
@@ -699,6 +762,9 @@
         rows_all = jnp.concatenate([hg[p, rows, :] for p in range(nx)], axis=1)
         out[rows, :] = dot1(rows_all, col_w[...]).astype(BF16)
 
+    for way in range(2):
+        for p in range(2):
+            last(way, p).wait_send()
     @pl.when(has_after)
     def _():
         for i in range(nx):
@@ -706,7 +772,8 @@
 
     for t in range(chunks):
         for way in range(2):
-            direct(way, t).wait_send()
+            if t < final:
+                direct(way, t).wait_send()
             relay(way, t).wait_send()
             h_direct(way, t).wait_send()
             h_relay(way, t).wait_send()
@@ -764,11 +831,17 @@
             pltpu.SMEM((heads,), F32),
             pltpu.SMEM((heads,), F32),
             pltpu.SMEM((heads,), F32),
+            pltpu.VMEM((chunks, BLK + PRE, width), F32),
+            pltpu.VMEM((chunks, BLK, width), F32),
+            pltpu.VMEM((chunks, 2, BLK, BLK), F32),
+            pltpu.VMEM((chunks, heads, BLK, BLK), F32),
+            pltpu.VMEM((chunks, heads, BLK, 2 * BLK), F32),
+            pltpu.VMEM((chunks, heads, BLK, 2 * BLK), F32),
             dma((13,)),
             dma((nx,)),
             dma((nx,)),
-            dma((2, chunks)),
-            dma((2, chunks)),
+            dma((2, chunks + 1)),
+            dma((2, chunks + 1)),
             dma((2, chunks)),
             dma((2, chunks)),
             dma((nx - 1,)),

time: 64.7 us -> 62.1 us (0.960)
  Pallas kernels: 63 us -> 61 us
    pallas_call x1, Pallas kernels: 63 us -> 61 us  [on_device(): pl.pallas_call(functools.partial(kernel, sizes), out_shape=pltpu.VMEM((to...]
where the time goes in v5:
time: 62.1 us; the launch traced here: 61.8 us
  Pallas kernels  61 us (98%)
  local copies, waits for them, and re-layouts  0.8 us (1%)
    pallas_call x1, Pallas kernels, on_device(): pl.pallas_call(functools.partial(kernel, sizes), out_shape=pltpu.VMEM((to...  61 us

profile of v5, /device:TPU:1, one launch (start us, length us, event | category | flops | bytes accessed | tf_op | source)
XLA Modules:
  0.0 61.8 jit_solution(5188112359930363257)
XLA Ops:
  0.0 61.0 %layer.1 = bf16[512,512]{1,0:T(8,128)(2,1)S(1)} custom-call(bf16[512,512]{1,0:T(8,128)(2,1)} %x_in.1, bf16[2048,256]{1,0:T(8,128)(2,1)} %wq.1, bf16[2048,256]{1,0:T(8,128)(2,1)} %wk.1, bf16[2048,256]{1,0:T(8,128)(2,1)} %wv.1, bf16[2048,256]{1,0:T(8,128)(2,1)} %wg.1, bf16[2,2048]{1,0:T(2,128)(2,1)} %bitcast.4, bf16[2,2048]{1,0:T(2,128)(2,1)} %bitcast.5, ...), custom_call_target="tpu_custom_call" | custom-call | tf_op jit(solution)/shard_map/layer/pallas_call | solution.py:807
  61.0 0.8 %copy.15 = bf16[512,512]{1,0:T(8,128)(2,1)} copy(bf16[512,512]{1,0:T(8,128)(2,1)S(1)} %layer.1) | data formatting | bytes 1048576

commit v6 on v5

--- a/solution.py
+++ b/solution.py
@@ -130,8 +130,6 @@
     decay_log,
     beta_bias,
     decay_bias,
-    kept_q,
-    kept_g,
     kept_total,
     kept_kt,
     kept_state,
@@ -182,11 +180,13 @@
     xg[:, 0:PRE, :] = jnp.zeros((nx, PRE, feats), BF16)
 
     weights = (wq, wk, wv, wg)
+    split = 2 * width + BLK
+    places = (split, 0, width, split + width)
     loads = [pltpu.make_async_copy(x_in, xg.at[x, pl.ds(PRE, tokens), :], load_sem.at[0])]
     loads[0].start()
     for i, w in enumerate(weights):
         cp = pltpu.make_async_copy(
-            w, w_all.at[:, pl.ds(i * width, width)], load_sem.at[1 + i]
+            w, w_all.at[:, pl.ds(places[i], width)], load_sem.at[1 + i]
         )
         cp.start()
         loads.append(cp)
@@ -343,7 +343,7 @@
         tile = jnp.where(wide_row == 2, d_rows[0:1], tile)
         tile = jnp.where(wide_row == 3, d_rows[1:2], tile)
         tile = jnp.concatenate([tile, jnp.zeros((BLK - 8, BLK), F32)], axis=0)
-        w_all[cols, 4 * width :] = jnp.transpose(tile).astype(BF16)
+        w_all[cols, 2 * width : split] = jnp.transpose(tile).astype(BF16)
 
     row_i = lax.broadcasted_iota(jnp.int32, (BLK, BLK), 0)
     col_i = lax.broadcasted_iota(jnp.int32, (BLK, BLK), 1)
@@ -373,19 +373,20 @@
             mixed = mixed + taps[s] * pltpu.roll(values, s, 0)
         return silu(mixed[PRE:])
 
-    def chunk(t):
-        start = pl.multiple_of(t * BLK, BLK)
+    def projected(t, begin, end):
+        start = t * BLK if isinstance(t, int) else pl.multiple_of(t * BLK, BLK)
         rows = pl.ds(start, BLK + PRE)
         xs = jnp.concatenate([xg[p, rows, :] for p in range(nx)], axis=1)
+        raw = dot1(xs, w_all[:, begin:end])
+        convolved = raw[:, : 2 * width] if begin == 0 else raw[:, :width]
         first = jnp.logical_and(here == 0, t == 0)
-        ext_row = lax.broadcasted_iota(jnp.int32, (BLK + PRE, 3 * width), 0)
-        raw = dot1(xs, w_all[...])
-        qkv = raw[:, 0 : 3 * width]
-        qkv = jnp.where(jnp.logical_and(first, ext_row < PRE), 0.0, qkv)
-        kept_q[t] = qkv[:, 0:width]
-        kept_g[t] = raw[PRE:, 3 * width : 4 * width]
-        mixed = mix_taps((1, 2), qkv[:, width:])
-        small = raw[PRE:, 4 * width :] + bias_row
+        ext_row = lax.broadcasted_iota(jnp.int32, convolved.shape, 0)
+        return raw, jnp.where(jnp.logical_and(first, ext_row < PRE), 0.0, convolved)
+
+    def chunk(t):
+        raw, kv = projected(t, 0, split)
+        mixed = mix_taps((1, 2), kv)
+        small = raw[PRE:, 2 * width :] + bias_row
         betas = sigmoid(small)
         steps = -rate_row * softplus(small)
         s_hi = steps.astype(BF16)
@@ -451,8 +452,9 @@
     def reading(t):
         start = t * BLK if isinstance(t, int) else pl.multiple_of(t * BLK, BLK)
         out_rows = pl.ds(start, BLK)
-        gates = silu(kept_g[t])
-        mixed = mix_taps((0,), kept_q[t])
+        raw, q_rows = projected(t, split, split + 2 * width)
+        gates = silu(raw[PRE:, width:])
+        mixed = mix_taps((0,), q_rows)
         total, total_t = kept_total[t, 0], kept_total[t, 1]
         for h in range(heads):
             cols = slice(h * BLK, (h + 1) * BLK)
@@ -831,8 +833,6 @@
             pltpu.SMEM((heads,), F32),
             pltpu.SMEM((heads,), F32),
             pltpu.SMEM((heads,), F32),
-            pltpu.VMEM((chunks, BLK + PRE, width), F32),
-            pltpu.VMEM((chunks, BLK, width), F32),
             pltpu.VMEM((chunks, 2, BLK, BLK), F32),
             pltpu.VMEM((chunks, heads, BLK, BLK), F32),
             pltpu.VMEM((chunks, heads, BLK, 2 * BLK), F32),

time: 62.1 us -> 62 us (level)
  no operation moved by 1% of the time
where the time goes in v6:
time: 62 us; the launch traced here: 61.4 us
  Pallas kernels  60.6 us (98%)
  local copies, waits for them, and re-layouts  0.8 us (1%)
    pallas_call x1, Pallas kernels, on_device(): pl.pallas_call(functools.partial(kernel, sizes), out_shape=pltpu.VMEM((to...  60.6 us

profile of v6, /device:TPU:1, one launch (start us, length us, event | category | flops | bytes accessed | tf_op | source)
XLA Modules:
  0.0 61.4 jit_solution(171856678545279896)
XLA Ops:
  0.0 60.6 %layer.1 = bf16[512,512]{1,0:T(8,128)(2,1)S(1)} custom-call(bf16[512,512]{1,0:T(8,128)(2,1)} %x_in.1, bf16[2048,256]{1,0:T(8,128)(2,1)} %wq.1, bf16[2048,256]{1,0:T(8,128)(2,1)} %wk.1, bf16[2048,256]{1,0:T(8,128)(2,1)} %wv.1, bf16[2048,256]{1,0:T(8,128)(2,1)} %wg.1, bf16[2,2048]{1,0:T(2,128)(2,1)} %bitcast.4, bf16[2,2048]{1,0:T(2,128)(2,1)} %bitcast.5, ...), custom_call_target="tpu_custom_call" | custom-call | tf_op jit(solution)/shard_map/layer/pallas_call | solution.py:809
  60.6 0.8 %copy.15 = bf16[512,512]{1,0:T(8,128)(2,1)} copy(bf16[512,512]{1,0:T(8,128)(2,1)S(1)} %layer.1) | data formatting | bytes 1048576
